TPU v7x, 32 devices: a whole 2x2x4 slice. The times are simulated.
32 devices in a mesh: theta: 8 (over z, core), gz: 4 (over y, x).
Axes of the slice: x: 2, y: 2, z: 4, core: 2. Of those that a mesh axis runs over, the one named last changes fastest.
Arguments:
- velocity: float32 [3, 512, 256, 128], P(None, 'theta', 'gz'), may hold values from -3 to 3
Outputs:
- viscosity_ratio: float32 [512, 256, 128], P('theta', 'gz')
- pressure_modes: float32 [2, 512, 256, 128], P(None, 'gz', 'theta')
All inputs are finite; a program needn't handle non-finite values.
Results may differ from a plain program's by a relative error of at most 0.0003.
Values sent between devices are 32-bit elements; how exact they have to be, the bound alone decides.
No kernel may reach another device: no remote copies, remote signals or barrier semaphores. Data moves between devices by JAX's collectives and lax.ppermute only.
A program may use at most 256 MiB of HBM per device.

v0:
```python
import functools
import math

import jax
import jax.numpy as jnp
import numpy as np
from jax import lax
from jax.experimental import pallas as pl
from jax.experimental.pallas import tpu as pltpu
from jax.sharding import PartitionSpec as P

pipe_length = 4.0 * math.pi
nu_molecular = 5e-05
time_step = 2.0
filter_ratio = 4.0
epsilon_den = 1e-06
CHUNKS = 2
VMEM_BYTES = 60 * 1024 * 1024
ANY = pl.BlockSpec(memory_space=pl.ANY)
VM = pl.BlockSpec(memory_space=pltpu.VMEM)


def params(limit=VMEM_BYTES):
    return pltpu.CompilerParams(vmem_limit_bytes=limit)


def round_up(value, unit):
    return (value + unit - 1) // unit * unit


class Grid:
    def __init__(self, velocity):
        self.nt = lax.axis_size("theta")
        self.ng = lax.axis_size("gz")
        _, self.T, self.Z, self.R = velocity.shape
        self.NTH = self.T * self.nt
        self.NZ = self.Z * self.ng
        self.kb = self.NZ // self.nt
        self.mb = self.NTH // self.ng
        self.chunks = CHUNKS
        while self.R % (self.chunks * self.ng):
            self.chunks //= 2
        self.rc = self.R // self.chunks
        self.rb = self.rc // self.ng
        self.kz = 0.5 * self.NZ / pipe_length
        self.kt = 0.5 * self.NTH / (2.0 * math.pi)

    def lanes(self):
        R = self.R
        index = lax.broadcasted_iota(jnp.int32, (8, R), 1)
        radius = (index.astype(jnp.float32) + 0.5) * (1.0 / R)
        inverse = 1.0 / radius
        up = jnp.where(index == R - 1, 0.0, 0.5 * R)
        down = jnp.where(index == 0, 0.0, 0.5 * R)
        return radius, inverse, up, down


def width_row(g):
    radius = (np.arange(g.R, dtype=np.float32) + np.float32(0.5)) * np.float32(1.0 / g.R)
    cell = radius.astype(np.float64) * (1.0 / g.R) * (2.0 * math.pi / g.NTH) * (pipe_length / g.NZ)
    return jnp.asarray(np.broadcast_to((np.cbrt(cell) ** 2).astype(np.float32), (8, g.R)))


def shift_up(f):
    return pltpu.roll(f, f.shape[-1] - 1, 1)


def shift_down(f):
    return pltpu.roll(f, 1, 1)


def strain_rows(pad, t, z, g, rows):
    inverse, up, down, kt = rows
    at = lambda c, dt, dz: pad[c, t + dt, z + dz : z + dz + 8, :]
    u = [at(c, 0, 0) for c in range(3)]
    radial = [shift_up(f) * up - shift_down(f) * down for f in u]
    turn = [(at(c, 1, 0) - at(c, -1, 0)) * kt for c in range(3)]
    axial = [(at(c, 0, 1) - at(c, 0, -1)) * g.kz for c in range(3)]
    ur, ut = u[0] * inverse, u[1] * inverse
    s = [
        radial[0],
        turn[1] + ur,
        axial[2],
        radial[1] - ut + turn[0],
        axial[0] + radial[2],
        turn[2] + axial[1],
    ]
    return u, s


def root(x):
    return x * lax.rsqrt(jnp.maximum(x, 1e-36))


def size_of(s):
    diag = s[0] * s[0] + s[1] * s[1] + s[2] * s[2]
    return root((diag + diag) + (s[3] * s[3] + s[4] * s[4] + s[5] * s[5]))


def fill_pad(g, v, tlo, thi, zlo, zhi, pad, sems):
    T, Z = g.T, g.Z
    copies = [
        pltpu.make_async_copy(v, pad.at[:, pl.ds(3, T), pl.ds(8, Z), :], sems.at[0]),
        pltpu.make_async_copy(tlo, pad.at[:, pl.ds(0, 3), pl.ds(8, Z), :], sems.at[1]),
        pltpu.make_async_copy(thi, pad.at[:, pl.ds(T + 3, 3), pl.ds(8, Z), :], sems.at[2]),
    ]
    for copy in copies:
        copy.start()
    rows = pad.reshape(3 * (T + 6) * (Z + 16), g.R)
    for c in range(3):
        for i in range(3):
            first = c * (T + 6) * (Z + 16)
            rows[pl.ds(first + 5 + i, T + 6, stride=Z + 16), :] = zlo[c, i]
            rows[pl.ds(first + 8 + Z + i, T + 6, stride=Z + 16), :] = zhi[c, i]
    for copy in copies:
        copy.wait()


PAIRS = ((0, 0), (1, 1), (2, 2), (0, 1), (0, 2), (1, 2))


def sums_kernel(g, v, tlo, thi, zlo, zhi, width, out, pad, raw, last, pair, acc, sems):
    fill_pad(g, v, tlo, thi, zlo, zhi, pad, sems)
    _, inverse, up, down = g.lanes()
    rows = (inverse, up, down, g.kt * inverse)
    acc[...] = jnp.zeros_like(acc)

    def step(t, carry):
        for zc in range(raw.shape[1] // 8):
            z = 7 + 8 * zc
            u, s = strain_rows(pad, t + 2, z, g, rows)
            size = size_of(s)
            here = pl.ds(8 * zc, 8)
            for n, (a, b) in enumerate(PAIRS):
                raw[n, here, :] = u[a] * u[b]
                raw[6 + n, here, :] = s[n]
                raw[12 + n, here, :] = size * s[n]
        live = t >= 2

        def smooth(n, load, zc):
            centre = load(1)
            h = (load(0) + load(2)) + (centre + centre)
            here = pl.ds(8 * zc, 8)
            two = last[n, here, :] + h
            result = pair[n, here, :] + two
            last[n, here, :] = h
            pair[n, here, :] = two
            return result

        for zc in range(g.Z // 8):
            mean = [
                smooth(c, lambda d, c=c: pad[c, t + 2, 7 + 8 * zc + d : 15 + 8 * zc + d, :], zc)
                for c in range(3)
            ]
            field = lambda n: smooth(
                3 + n, lambda d: raw[n, 8 * zc + d : 8 * zc + d + 8, :], zc
            )
            scaled = [m * 0.0625 for m in mean]
            leonard = [field(n) - scaled[a] * mean[b] for n, (a, b) in enumerate(PAIRS)]
            calm = [field(6 + n) for n in range(6)]
            size = size_of(calm) * (filter_ratio / 16.0)
            model = [size * calm[n] - field(12 + n) for n in range(6)]
            numer = leonard[0] * model[0]
            for n in range(1, 6):
                numer = numer + leonard[n] * model[n]
            diag = model[0] * model[0] + model[1] * model[1] + model[2] * model[2]
            side = model[3] * model[3] + model[4] * model[4] + model[5] * model[5]
            acc[0] += jnp.where(live, numer, 0.0)
            acc[1] += jnp.where(live, diag + 0.5 * side, 0.0)
        return carry

    lax.fori_loop(0, g.T + 2, step, 0)
    w = width[...] * (2.0 / 16.0)
    numer = jnp.sum(acc[0], axis=0, keepdims=True) * (w[:1] * (1.0 / 16.0))
    denom = jnp.sum(acc[1], axis=0, keepdims=True) * (w[:1] * w[:1])
    index = lax.broadcasted_iota(jnp.int32, (8, g.R), 0)
    out[...] = jnp.where(index == 0, numer, jnp.where(index == 1, denom, 0.0))


def source_kernel(g, v, tlo, thi, zlo, zhi, width, sums, ratio, *rest):
    outs = rest[: g.chunks * g.ng]
    pad, tau, eddy, vt, vz, src, flip, sems, osems = rest[g.chunks * g.ng :]
    T, Z, R = g.T, g.Z, g.R
    fill_pad(g, v, tlo, thi, zlo, zhi, pad, sems)
    radius, inverse, up, down = g.lanes()
    rows = (inverse, up, down, g.kt * inverse)
    kt = rows[3]
    total = jnp.sum(sums[...], axis=0)
    coefficient = total[0:1] / (total[1:2] + epsilon_den)
    strength = jnp.broadcast_to(coefficient, (8, R)) * width[...]

    def stress_row(t, carry):
        for zc in range(eddy.shape[1] // 8):
            z = 6 + 8 * zc
            _, s = strain_rows(pad, t + 1, z, g, rows)
            e = strength * size_of(s)
            here = pl.ds(8 * zc, 8)
            eddy[t, here, :] = e * (1.0 / nu_molecular)
            side = time_step * (nu_molecular + e)
            main = side + side
            for n in range(3):
                tau[n, t, here, :] = main * s[n]
                tau[3 + n, t, here, :] = side * s[3 + n]
        return carry

    lax.fori_loop(0, T + 4, stress_row, 0)

    def slab(n, t, z):
        return tau[n, t, z : z + 8, :]

    def radial(f):
        return shift_up(f) * up - shift_down(f) * down

    def turn_row(a, carry):
        t = a + 1
        for zc in range(Z // 8):
            z = 2 + 8 * zc
            rt = slab(3, t, z)
            force = (
                radial(rt)
                + (slab(1, t + 1, z) - slab(1, t - 1, z)) * kt
                + (slab(5, t, z + 1) - slab(5, t, z - 1)) * g.kz
                + rt * (inverse + inverse)
            )
            vt[a, pl.ds(8 * zc, 8), :] = pad[1, a + 2, 8 + 8 * zc : 16 + 8 * zc, :] + force
        return carry

    lax.fori_loop(0, T + 2, turn_row, 0)
    r_up = shift_up(radius) * inverse * up
    r_down = shift_down(radius) * inverse * down

    def source_row(a, carry):
        t = a + 2
        for zc in range(vz.shape[0] // 8):
            z = 1 + 8 * zc
            rz = slab(4, t, z)
            force = (
                radial(rz)
                + (slab(5, t + 1, z) - slab(5, t - 1, z)) * kt
                + (slab(2, t, z + 1) - slab(2, t, z - 1)) * g.kz
                + rz * inverse
            )
            vz[pl.ds(8 * zc, 8), :] = pad[2, a + 3, 7 + 8 * zc : 15 + 8 * zc, :] + force
        for zc in range(Z // 8):
            z = 2 + 8 * zc
            here = pl.ds(8 * zc, 8)
            rr = slab(0, t, z)
            force = (
                radial(rr)
                + (slab(3, t + 1, z) - slab(3, t - 1, z)) * kt
                + (slab(4, t, z + 1) - slab(4, t, z - 1)) * g.kz
                + (rr - slab(1, t, z)) * inverse
            )
            vr = pad[0, a + 3, 8 + 8 * zc : 16 + 8 * zc, :] + force
            src[a, here, :] = (
                shift_up(vr) * r_up
                - shift_down(vr) * r_down
                + (vt[a + 2, here, :] - vt[a, here, :]) * kt
                + (vz[8 * zc + 2 : 8 * zc + 10, :] - vz[8 * zc : 8 * zc + 8, :]) * g.kz
            )
            ratio[a, here, :] = eddy[t, z : z + 8, :]
        return carry

    lax.fori_loop(0, T, source_row, 0)
    flat = src.reshape(T * src.shape[1], R)
    turned = flip.reshape(R * flip.shape[1], 2 * T)

    def flip_step(p, carry):
        even = flat[pl.ds(2 * p, T, stride=src.shape[1]), :]
        odd = flat[pl.ds(2 * p + 1, T, stride=src.shape[1]), :]
        turned[pl.ds(p, R, stride=flip.shape[1]), :] = jnp.concatenate([even, odd], axis=0).T
        return carry

    lax.fori_loop(0, Z // 2, flip_step, 0)
    me = lax.axis_index("gz")
    copies = []
    for c in range(g.chunks):
        for s in range(g.ng):
            first = c * g.rc + lax.rem(me + s, g.ng) * g.rb
            n = c * g.ng + s
            copies.append(
                pltpu.make_async_copy(
                    flip.at[pl.ds(first, g.rb), pl.ds(0, Z // 2), :], outs[n], osems.at[n]
                )
            )
    for copy in copies:
        copy.start()
    for copy in copies:
        copy.wait()


def split(x):
    parts = []
    for _ in range(2):
        parts.append(x.astype(jnp.bfloat16))
        x = x - parts[-1].astype(jnp.float32)
    return parts + [x.astype(jnp.bfloat16)]


def split_table(x):
    parts = []
    for _ in range(2):
        high = lax.reduce_precision(x, 8, 7)
        parts.append(high.astype(jnp.bfloat16))
        x = x - high
    return parts + [x.astype(jnp.bfloat16)]


def dot6(a, b):
    dot = functools.partial(jnp.dot, preferred_element_type=jnp.float32)
    small = dot(a[1], b[1]) + dot(a[2], b[0]) + dot(a[0], b[2])
    return dot(a[0], b[0]) + (dot(a[1], b[0]) + dot(a[0], b[1]) + small)


def axial_kernel(g, *refs):
    blocks, tables = refs[: g.ng], refs[g.ng : g.ng + 3]
    outs = refs[g.ng + 3 : g.ng + 3 + g.nt]
    left = refs[g.ng + 3 + g.nt :]
    T, zp, kb = g.T, g.Z // 2, g.kb
    mine, other = lax.axis_index("gz"), lax.axis_index("theta")
    for s in range(g.ng):
        source = lax.rem(mine + g.ng - s, g.ng)
        for d in range(g.nt):
            target = lax.rem(other + d, g.nt)
            here = (pl.ds(d * kb, kb), pl.ds(4 * zp * s, 4 * zp))
            for n in range(3):
                left[n][here] = tables[n][source, target]
    per = 2 if g.rb % 2 == 0 else 1
    first = lax.broadcasted_iota(jnp.int32, (zp, 2 * T), 1) < T

    def column(r):
        parts = []
        for s in range(g.ng):
            x = blocks[s][r]
            y = jnp.concatenate([x[:, T:], x[:, :T]], axis=1)
            for f in (x, y):
                parts.append(jnp.where(first, f, 0.0))
                parts.append(jnp.where(first, 0.0, f))
        return jnp.concatenate(parts, axis=0)

    def step(i, carry):
        right = jnp.concatenate([column(per * i + q) for q in range(per)], axis=1)
        result = dot6([w[...] for w in left], split(right))
        for q in range(per):
            for d in range(g.nt):
                outs[d][per * i + q] = result[d * kb : (d + 1) * kb, q * 2 * T : (q + 1) * 2 * T]
        return carry

    lax.fori_loop(0, g.rb // per, step, 0)


def turn_kernel(g, *refs):
    blocks, tables = refs[: g.nt], refs[g.nt : g.nt + 3]
    outs = refs[g.nt + 3 : g.nt + 3 + g.ng]
    mine, other = lax.axis_index("theta"), lax.axis_index("gz")
    rows = g.rb * g.kb
    left = split(jnp.concatenate([b[...].reshape(rows, 2 * g.T) for b in blocks], axis=1))
    for d in range(g.ng):
        target = lax.rem(other + d, g.ng)
        source = [lax.rem(mine + g.nt - s, g.nt) for s in range(g.nt)]
        right = [jnp.concatenate([w[target, s] for s in source], axis=0) for w in tables]
        result = dot6(left, right)
        for c in range(2):
            part = result[:, c * g.mb : (c + 1) * g.mb]
            outs[d][c] = part.reshape(g.rb, g.kb, g.mb)


def solve_kernel(g, *refs):
    count = g.chunks * g.ng
    blocks, coefs, out = refs[:count], refs[count], refs[count + 1]
    data, factor, flip, sems, osems = refs[count + 2 :]
    R, kb, mb = g.R, g.kb, g.mb
    mine, other = lax.axis_index("gz"), lax.axis_index("theta")
    copies = []
    for c in range(g.chunks):
        for s in range(g.ng):
            first = c * g.rc + lax.rem(mine + g.ng - s, g.ng) * g.rb
            n = c * g.ng + s
            copies.append(
                pltpu.make_async_copy(
                    blocks[n], data.at[:, pl.ds(first, g.rb), pl.ds(0, kb), :], sems.at[n]
                )
            )
    for copy in copies:
        copy.start()
    for copy in copies:
        copy.wait()
    m = mine * mb + lax.broadcasted_iota(jnp.int32, (kb, mb), 1)
    k = other * kb + lax.broadcasted_iota(jnp.int32, (kb, mb), 0)
    a = jnp.minimum(m, g.NTH - m).astype(jnp.float32)
    q = jnp.minimum(k, g.NZ - k).astype(jnp.float32) * (2.0 * math.pi / pipe_length)
    a2, q2 = a * a, q * q
    zero = jnp.zeros((kb, mb), jnp.float32)

    def forward(r, carry):
        cp, re, im = carry
        lower, upper, centre, inv2 = (coefs[n, r] for n in range(4))
        w = 1.0 / ((centre - q2) - a2 * inv2 - lower * cp)
        cp = upper * w
        re = (data[0, r, :kb, :] - lower * re) * w
        im = (data[1, r, :kb, :] - lower * im) * w
        factor[r] = cp
        data[0, r, :kb, :] = re
        data[1, r, :kb, :] = im
        return cp, re, im

    lax.fori_loop(0, R, forward, (zero, zero, zero), unroll=2)

    def backward(i, carry):
        re, im = carry
        r = R - 1 - i
        cp = factor[r]
        re = data[0, r, :kb, :] - cp * re
        im = data[1, r, :kb, :] - cp * im
        data[0, r, :kb, :] = re
        data[1, r, :kb, :] = im
        return re, im

    lax.fori_loop(0, R, backward, (zero, zero), unroll=2)
    flat = data.reshape(2 * R * data.shape[2], mb)
    turned = flip.reshape(2 * mb * flip.shape[2], R)
    stores = []
    for c in range(2):

        def flip_step(i, carry):
            rows = flat[pl.ds(c * R * data.shape[2] + i, R, stride=data.shape[2]), :]
            turned[pl.ds(c * mb * flip.shape[2] + i, mb, stride=flip.shape[2]), :] = rows.T
            return carry

        lax.fori_loop(0, kb, flip_step, 0)
        copy = pltpu.make_async_copy(flip.at[c, :, pl.ds(0, kb), :], out.at[c], osems.at[c])
        copy.start()
        stores.append(copy)
    for copy in stores:
        copy.wait()


def exchange(blocks, axis):
    count = len(blocks)
    return [blocks[0]] + [
        lax.ppermute(blocks[s], axis, [(i, (i + s) % count) for i in range(count)])
        for s in range(1, count)
    ]


def halo(g, v):
    T, Z = g.T, g.Z

    def pair(low, high, axis, count):
        forward = [(i, (i + 1) % count) for i in range(count)]
        backward = [(target, source) for source, target in forward]
        return lax.ppermute(high, axis, forward), lax.ppermute(low, axis, backward)

    tlo, thi = pair(v[:, :3], v[:, T - 3 :], "theta", g.nt)
    face = lambda first: jnp.concatenate(
        [f[:, :, first : first + 3].transpose(0, 2, 1, 3) for f in (tlo, v, thi)], axis=2
    )
    zlo, zhi = pair(face(0), face(Z - 3), "gz", g.ng)
    return tlo, thi, zlo, zhi


def axial_table(g):
    z, k = np.arange(g.NZ), np.arange(g.NZ)
    angle = 2.0 * math.pi * ((k[:, None] * z[None, :]) % g.NZ) / g.NZ
    scale = 1.0 / math.sqrt(g.NTH * g.NZ)
    cos = (np.cos(angle) * scale).reshape(g.nt, g.kb, g.ng, g.Z // 2, 2)
    sin = (-np.sin(angle) * scale).reshape(g.nt, g.kb, g.ng, g.Z // 2, 2)
    parts = [cos[..., 0], sin[..., 1], cos[..., 1], sin[..., 0]]
    table = np.stack(parts, axis=3).reshape(g.nt, g.kb, g.ng, 2 * g.Z)
    return split_table(jnp.asarray(table.transpose(2, 0, 1, 3).astype(np.float32)))


def turn_table(g):
    t, m = np.arange(g.T), np.arange(g.NTH)
    base = 2.0 * math.pi * ((t[:, None] * m[None, :]) % g.NTH) / g.NTH
    skip = 2.0 * math.pi * ((np.arange(g.nt)[:, None] * g.T * m[None, :]) % g.NTH) / g.NTH
    f32 = lambda x: jnp.asarray(x.astype(np.float32))
    fold = lambda x: x.reshape(x.shape[0], g.ng, g.mb).transpose(1, 0, 2)
    c0, s0 = f32(fold(np.cos(base)))[:, None], f32(fold(np.sin(base)))[:, None]
    c1, s1 = f32(fold(np.cos(skip)))[:, :, None], f32(fold(np.sin(skip)))[:, :, None]
    cos = c0 * c1 - s0 * s1
    sin = s0 * c1 + c0 * s1
    top = jnp.concatenate([cos, -sin], axis=-1)
    bottom = jnp.concatenate([sin, cos], axis=-1)
    return split_table(jnp.concatenate([top, bottom], axis=-2))


def solve_coefs(g):
    R = g.R
    radius = (np.arange(R) + 0.5) / R
    lower = (radius - 0.5 / R) / radius * (R * R)
    upper = (radius + 0.5 / R) / radius * (R * R)
    last = np.arange(R) == R - 1
    centre = -(lower + upper) - np.where(last, upper, 0.0)
    upper = np.where(last, 0.0, upper)
    return jnp.asarray(np.stack([lower, upper, centre, 1.0 / radius**2]).astype(np.float32))


def body(velocity):
    g = Grid(velocity)
    T, Z, R, rb, kb, mb = g.T, g.Z, g.R, g.rb, g.kb, g.mb
    f32 = jnp.float32
    shape = lambda *s: jax.ShapeDtypeStruct(s, f32)
    buf = lambda *s: pltpu.VMEM(s, f32)
    dma = pltpu.SemaphoreType.DMA
    edges = halo(g, velocity)
    width = width_row(g)
    pad = buf(3, T + 6, Z + 16, R)
    halo_specs = [ANY, ANY, ANY, VM, VM, VM]
    part = pl.pallas_call(
        functools.partial(sums_kernel, g),
        out_shape=shape(8, R),
        in_specs=halo_specs,
        out_specs=VM,
        scratch_shapes=[
            pad,
            buf(18, round_up(Z + 2, 8), R),
            buf(21, Z, R),
            buf(21, Z, R),
            buf(2, 8, R),
            dma((3,)),
        ],
        compiler_params=params(),
        name="germano_sums",
    )(velocity, *edges, width)
    count = g.nt * g.ng
    sums = lax.all_to_all(
        jnp.broadcast_to(part[None], (count, 8, R)), ("theta", "gz"), 0, 0, tiled=True
    )
    outs = pl.pallas_call(
        functools.partial(source_kernel, g),
        out_shape=[shape(T, Z, R)] + [shape(rb, Z // 2, 2 * T)] * (g.chunks * g.ng),
        in_specs=halo_specs + [VM],
        out_specs=[VM] + [ANY] * (g.chunks * g.ng),
        scratch_shapes=[
            pad,
            buf(6, T + 4, round_up(Z + 4, 8) + 8, R),
            buf(T + 4, round_up(Z + 4, 8), R),
            buf(T + 2, Z, R),
            buf(round_up(Z + 2, 8), R),
            buf(T, Z + 8, R),
            buf(R, Z // 2 + 8, 2 * T),
            dma((3,)),
            dma((g.chunks * g.ng,)),
        ],
        compiler_params=params(),
        name="source",
    )(velocity, *edges, width, sums)
    ratio, pieces = outs[0], outs[1:]
    axial_tables = axial_table(g)
    turn_tables = turn_table(g)
    modes = []
    for c in range(g.chunks):
        lines = exchange(pieces[c * g.ng : (c + 1) * g.ng], "gz")
        axial = pl.pallas_call(
            functools.partial(axial_kernel, g),
            out_shape=[shape(rb, kb, 2 * T)] * g.nt,
            in_specs=[VM] * (g.ng + 3),
            out_specs=[VM] * g.nt,
            scratch_shapes=[pltpu.VMEM((g.NZ, 2 * g.NZ), jnp.bfloat16)] * 3,
            compiler_params=params(24 * 1024 * 1024),
            name="axial_modes",
        )(*lines, *axial_tables)
        cycles = exchange(axial, "theta")
        turned = pl.pallas_call(
            functools.partial(turn_kernel, g),
            out_shape=[shape(2, rb, kb, mb)] * g.ng,
            in_specs=[VM] * (g.nt + 3),
            out_specs=[VM] * g.ng,
            compiler_params=params(40 * 1024 * 1024),
            name="turn_modes",
        )(*cycles, *turn_tables)
        modes += exchange(turned, "gz")
    pressure = pl.pallas_call(
        functools.partial(solve_kernel, g),
        out_shape=shape(2, mb, kb, R),
        in_specs=[ANY] * len(modes) + [pl.BlockSpec(memory_space=pltpu.SMEM)],
        out_specs=ANY,
        scratch_shapes=[
            buf(2, R, kb + 8, mb),
            buf(R, kb, mb),
            buf(2, mb, kb + 8, R),
            dma((len(modes),)),
            dma((2,)),
        ],
        compiler_params=params(40 * 1024 * 1024),
        name="solve_modes",
    )(*modes, solve_coefs(g))
    return (ratio, pressure)


def solution(mesh):
    return jax.shard_map(
        body,
        mesh=mesh,
        in_specs=(P(None, "theta", "gz", None),),
        out_specs=(P("theta", "gz", None), P(None, "gz", "theta", None)),
        check_vma=False,
    )
```

profile of v0, /device:TPU:15, one launch (start us, length us, event | category | flops | bytes accessed | tf_op | source)
XLA Modules:
  0.0 280.8 jit_solution(10100685287093431348)
XLA Ops:
  5.7 4.2 %collective-permute-done = f32[3,3,64,128]{3,1,2,0:T(4,128)S(1)} collective-permute-done((f32[3,3,64,128]{3,1,2,0:T(4,128)S(1)}, f32[3,3,64,128]{3,1,2,0:T(4,128)S(1)}, u32[]{:S(2)}, u32[]{:S(2)}) %collective-permute-start) | collective-permute-done | bytes 294944 | tf_op jit(solution)/shard_map/ppermute | solution.py:452
  10.0 4.2 %collective-permute-done.1 = f32[3,3,64,128]{3,1,2,0:T(4,128)S(1)} collective-permute-done((f32[3,3,64,128]{3,1,2,0:T(4,128)S(1)}, f32[3,3,64,128]{3,1,2,0:T(4,128)S(1)}, u32[]{:S(2)}, u32[]{:S(2)}) %collective-permute-start.1) | collective-permute-done | bytes 294944 | tf_op jit(solution)/shard_map/ppermute | solution.py:452
  18.3 6.6 %collective-permute-done.3.zhi = f32[3,3,70,128]{3,2,1,0:T(8,128)S(1)} collective-permute-done((f32[3,3,70,128]{3,2,1,0:T(8,128)S(1)}, f32[3,3,70,128]{3,2,1,0:T(8,128)S(1)}, u32[]{:S(2)}, u32[]{:S(2)}) %collective-permute-start.3) | collective-permute-done | bytes 322592 | tf_op jit(solution)/shard_map/ppermute | solution.py:452
  24.9 6.2 %collective-permute-done.2.zlo = f32[3,3,70,128]{3,2,1,0:T(8,128)S(1)} collective-permute-done((f32[3,3,70,128]{3,2,1,0:T(8,128)S(1)}, f32[3,3,70,128]{3,2,1,0:T(8,128)S(1)}, u32[]{:S(2)}, u32[]{:S(2)}) %collective-permute-start.2) | collective-permute-done | bytes 322592 | tf_op jit(solution)/shard_map/ppermute | solution.py:452
  31.8 31.3 %germano_sums.1 = f32[8,128]{1,0:T(8,128)} custom-call(f32[3,64,64,128]{3,2,1,0:T(8,128)} %v.3, f32[3,3,64,128]{3,2,1,0:T(8,128)} %copy.16.tlo, f32[3,3,64,128]{3,2,1,0:T(8,128)} %copy.17.thi, f32[3,3,70,128]{3,2,1,0:T(8,128)} %copy-done.7, f32[3,3,70,128]{3,2,1,0:T(8,128)} %copy-done.6, f32[8,128]{1,0:T(8,128)} %jit_solution_.3.width), custom_call_target="tpu_custom_call" | custom-call | tf_op jit(solution)/shard_map/germano_sums/pallas_call | solution.py:510
  63.8 10.5 %all_to_all.5.sums = f32[32,8,128]{2,1,0:T(8,128)} all-to-all(f32[32,8,128]{2,1,0:T(8,128)S(1)} %broadcast_in_dim.2), channel_id=1, replica_groups=mesh['theta'=8,'gz'=4] {'theta','gz'}, dimensions={0} | all-to-all | bytes 262144 | tf_op jit(solution)/shard_map/all_to_all | solution.py:527
  74.4 36.8 %source.1 = (f32[64,64,128]{2,1,0:T(8,128)}, f32[16,32,128]{2,1,0:T(8,128)}, f32[16,32,128]{2,1,0:T(8,128)}, f32[16,32,128]{2,1,0:T(8,128)}, f32[16,32,128]{2,1,...) custom-call(f32[3,64,64,128]{3,2,1,0:T(8,128)} %v.3, ...), custom_call_target="tpu_custom_call" | custom-call | tf_op jit(solution)/shard_map/source/pallas_call | solution.py:530
  118.7 2.3 collective-permute-start.6
  121.0 4.3 %collective-permute-done.19.refs_3_ = f32[16,32,128]{2,1,0:T(8,128)S(1)} collective-permute-done((f32[16,32,128]{2,1,0:T(8,128)}, f32[16,32,128]{2,1,0:T(8,128)S(1)}, u32[]{:S(2)}, u32[]{:S(2)}) %collective-permute-start.19) | collective-permute-done | bytes 262176 | tf_op jit(solution)/shard_map/ppermute | solution.py:441
  126.3 5.3 %axial_modes.3 = (f32[16,32,128]{2,1,0:T(8,128)S(1)}, f32[16,32,128]{2,1,0:T(8,128)S(1)}, f32[16,32,128]{2,1,0:T(8,128)S(1)}, f32[16,32,128]{2,1,0:T(8,128)S(1)}...) custom-call(f32[16,32,128]{2,1,0:T(8,128)S(1)} %copy-done.4, ...), custom_call_target="tpu_custom_call" | custom-call | tf_op jit(solution)/shard_map/axial_modes/pallas_call | solution.py:555
  131.6 4.1 %collective-permute-start.20 = (f32[16,32,128]{2,1,0:T(8,128)S(1)}, f32[16,32,128]{2,1,0:T(8,128)S(1)}, u32[]{:S(2)}, u32[]{:S(2)}) collective-permute-start(f32[16,32,128]{2,1,0:T(8,128)S(1)} %get-tuple-element.57), channel_id=1, source_target_pairs={{0,4},{4,8},{8,12},{12,16},{16,20},{20,24},{24,28},{28,0},{1,5},{5... | collective-permute-start | bytes 786440 | tf_op jit(solution)/shard_map/ppermute | solution.py:441
  143.4 4.9 %collective-permute-done.21.refs_2_ = f32[16,32,128]{2,1,0:T(8,128)S(1)} collective-permute-done((f32[16,32,128]{2,1,0:T(8,128)S(1)}, f32[16,32,128]{2,1,0:T(8,128)S(1)}, u32[]{:S(2)}, u32[]{:S(2)}) %collective-permute-start.21) | collective-permute-done | bytes 262176 | tf_op jit(solution)/shard_map/ppermute | solution.py:441
  149.6 5.3 %axial_modes.2 = (f32[16,32,128]{2,1,0:T(8,128)S(1)}, f32[16,32,128]{2,1,0:T(8,128)S(1)}, f32[16,32,128]{2,1,0:T(8,128)S(1)}, f32[16,32,128]{2,1,0:T(8,128)S(1)}...) custom-call(f32[16,32,128]{2,1,0:T(8,128)S(1)} %copy-done.3, ...), custom_call_target="tpu_custom_call" | custom-call | tf_op jit(solution)/shard_map/axial_modes/pallas_call | solution.py:555
  154.9 28.4 %collective-permute-done.22.refs_3_ = f32[16,32,128]{2,1,0:T(8,128)S(1)} collective-permute-done((f32[16,32,128]{2,1,0:T(8,128)S(1)}, f32[16,32,128]{2,1,0:T(8,128)S(1)}, u32[]{:S(2)}, u32[]{:S(2)}) %collective-permute-start.22) | collective-permute-done | bytes 262176 | tf_op jit(solution)/shard_map/ppermute | solution.py:441
  183.3 5.6 %collective-permute-done.23.refs_4_ = f32[16,32,128]{2,1,0:T(8,128)S(1)} collective-permute-done((f32[16,32,128]{2,1,0:T(8,128)S(1)}, f32[16,32,128]{2,1,0:T(8,128)S(1)}, u32[]{:S(2)}, u32[]{:S(2)}) %collective-permute-start.23) | collective-permute-done | bytes 262176 | tf_op jit(solution)/shard_map/ppermute | solution.py:441
  189.2 6.7 %turn_modes.3 = (f32[2,16,32,128]{3,2,1,0:T(8,128)S(1)}, f32[2,16,32,128]{3,2,1,0:T(8,128)S(1)}, f32[2,16,32,128]{3,2,1,0:T(8,128)S(1)}, f32[2,16,32,128]{3,2,1,0:T(8,128)S(1)}) custom-call(f32[16,32,128]{2,1,0:T(8,128)S(1)} %get-tuple-element.56.refs_0_, f32[16,32,128]{2,1,0:T(8,128)S(1)} %collective-permute-done.20.refs_1_, ...), custom_call_target="tpu_custom_call" | custom-call | tf_op jit(solution)/shard_map/turn_modes/pallas_call | solution.py:565
  196.6 4.4 %collective-permute-start.13 = (f32[16,32,128]{2,1,0:T(8,128)S(1)}, f32[16,32,128]{2,1,0:T(8,128)S(1)}, u32[]{:S(2)}, u32[]{:S(2)}) collective-permute-start(f32[16,32,128]{2,1,0:T(8,128)S(1)} %get-tuple-element.47), channel_id=1, source_target_pairs={{0,28},{4,0},{8,4},{12,8},{16,12},{20,16},{24,20},{28,24},{1,29},{... | collective-permute-start | bytes 786440 | tf_op jit(solution)/shard_map/ppermute | solution.py:441
  203.0 4.4 %collective-permute-start.8 = (f32[16,32,128]{2,1,0:T(8,128)S(1)}, f32[16,32,128]{2,1,0:T(8,128)S(1)}, u32[]{:S(2)}, u32[]{:S(2)}) collective-permute-start(f32[16,32,128]{2,1,0:T(8,128)S(1)} %get-tuple-element.42), channel_id=1, source_target_pairs={{0,8},{4,12},{8,16},{12,20},{16,24},{20,28},{24,0},{28,4},{1,9},{5... | collective-permute-start | bytes 786440 | tf_op jit(solution)/shard_map/ppermute | solution.py:441
  207.4 13.7 %collective-permute-done.12.refs_6_ = f32[16,32,128]{2,1,0:T(8,128)S(1)} collective-permute-done((f32[16,32,128]{2,1,0:T(8,128)S(1)}, f32[16,32,128]{2,1,0:T(8,128)S(1)}, u32[]{:S(2)}, u32[]{:S(2)}) %collective-permute-start.12) | collective-permute-done | bytes 262176 | tf_op jit(solution)/shard_map/ppermute | solution.py:441
  221.1 8.1 %collective-permute-done.13.refs_7_ = f32[16,32,128]{2,1,0:T(8,128)S(1)} collective-permute-done((f32[16,32,128]{2,1,0:T(8,128)S(1)}, f32[16,32,128]{2,1,0:T(8,128)S(1)}, u32[]{:S(2)}, u32[]{:S(2)}) %collective-permute-start.13) | collective-permute-done | bytes 262176 | tf_op jit(solution)/shard_map/ppermute | solution.py:441
  230.2 6.7 %turn_modes.2 = (f32[2,16,32,128]{3,2,1,0:T(8,128)S(1)}, f32[2,16,32,128]{3,2,1,0:T(8,128)S(1)}, f32[2,16,32,128]{3,2,1,0:T(8,128)S(1)}, f32[2,16,32,128]{3,2,1,0:T(8,128)S(1)}) custom-call(f32[16,32,128]{2,1,0:T(8,128)S(1)} %get-tuple-element.40.refs_0_, f32[16,32,128]{2,1,0:T(8,128)S(1)} %collective-permute-done.7.refs_1_, ...), custom_call_target="tpu_custom_call" | custom-call | tf_op jit(solution)/shard_map/turn_modes/pallas_call | solution.py:565
  239.8 9.0 %collective-permute-done.28.refs_6_ = f32[2,16,32,128]{3,2,1,0:T(8,128)S(1)} collective-permute-done((f32[2,16,32,128]{3,2,1,0:T(8,128)S(1)}, f32[2,16,32,128]{3,2,1,0:T(8,128)S(1)}, u32[]{:S(2)}, u32[]{:S(2)}) %collective-permute-start.28) | collective-permute-done | bytes 524320 | tf_op jit(solution)/shard_map/ppermute | solution.py:441
  250.6 18.8 %collective-permute-done.15.refs_2_ = f32[2,16,32,128]{3,2,1,0:T(8,128)S(1)} collective-permute-done((f32[2,16,32,128]{3,2,1,0:T(8,128)S(1)}, f32[2,16,32,128]{3,2,1,0:T(8,128)S(1)}, u32[]{:S(2)}, u32[]{:S(2)}) %collective-permute-start.15) | collective-permute-done | bytes 524320 | tf_op jit(solution)/shard_map/ppermute | solution.py:441
  269.4 11.2 %solve_modes.1 = f32[2,128,32,128]{3,2,1,0:T(8,128)} custom-call(f32[2,16,32,128]{3,2,1,0:T(8,128)S(1)} %get-tuple-element.48.refs_0_, f32[2,16,32,128]{3,2,1,0:T(8,128)S(1)} %collective-permute-done.14.refs_1_, f32[2,16,32,128]{3,2,1,0:T(8,128)S(1)} %collective-permute-done.15.refs_2_, f32[2,16,32,128]{3,2,1,0:T(8,128)S(1)} %collective-permute-done.16.refs_3_, ...), custom_call_target="tpu_custom_call" | custom-call | tf_op jit(solution)/shard_map/solve_modes/pallas_call | solution.py:574
  (86 shorter events, 36.8 us)
Async XLA Ops:
  14.2 10.6 %collective-permute-start.3 = (f32[3,3,70,128]{3,2,1,0:T(8,128)S(1)}, f32[3,3,70,128]{3,2,1,0:T(8,128)S(1)}, u32[]{:S(2)}, u32[]{:S(2)}) collective-permute-start(f32[3,3,70,128]{3,2,1,0:T(8,128)S(1)} %pad_maximum_fusion.1), channel_id=1, source_target_pairs={{1,0},{2,1},{3,2},{0,3},{5,4},{6,5},{7,6},{4,7},{9,8},{10,9},{11,1... | collective-permute-start | bytes 967688 | tf_op jit(solution)/shard_map/ppermute | solution.py:452
  14.6 16.4 %collective-permute-start.2 = (f32[3,3,70,128]{3,2,1,0:T(8,128)S(1)}, f32[3,3,70,128]{3,2,1,0:T(8,128)S(1)}, u32[]{:S(2)}, u32[]{:S(2)}) collective-permute-start(f32[3,3,70,128]{3,2,1,0:T(8,128)S(1)} %pad_maximum_fusion), channel_id=1, source_target_pairs={{0,1},{1,2},{2,3},{3,0},{4,5},{5,6},{6,7},{7,4},{8,9},{9,10},{10,1... | collective-permute-start | bytes 967688 | tf_op jit(solution)/shard_map/ppermute | solution.py:452
  113.5 11.8 %collective-permute-start.19 = (f32[16,32,128]{2,1,0:T(8,128)}, f32[16,32,128]{2,1,0:T(8,128)S(1)}, u32[]{:S(2)}, u32[]{:S(2)}) collective-permute-start(f32[16,32,128]{2,1,0:T(8,128)} %get-tuple-element.55), channel_id=1, source_target_pairs={{0,3},{1,0},{2,1},{3,2},{4,7},{5,4},{6,5},{7,6},{8,11},{9,8},{10,9... | collective-permute-start | bytes 786440 | tf_op jit(solution)/shard_map/ppermute | solution.py:441
  113.7 23.3 %collective-permute-start.4 = (f32[16,32,128]{2,1,0:T(8,128)}, f32[16,32,128]{2,1,0:T(8,128)S(1)}, u32[]{:S(2)}, u32[]{:S(2)}) collective-permute-start(f32[16,32,128]{2,1,0:T(8,128)} %get-tuple-element.37), channel_id=1, source_target_pairs={{0,1},{1,2},{2,3},{3,0},{4,5},{5,6},{6,7},{7,4},{8,9},{9,10},{10,1... | collective-permute-start | bytes 786440 | tf_op jit(solution)/shard_map/ppermute | solution.py:441
  115.9 23.5 %collective-permute-start.5 = (f32[16,32,128]{2,1,0:T(8,128)}, f32[16,32,128]{2,1,0:T(8,128)S(1)}, u32[]{:S(2)}, u32[]{:S(2)}) collective-permute-start(f32[16,32,128]{2,1,0:T(8,128)} %get-tuple-element.38), channel_id=1, source_target_pairs={{0,2},{1,3},{2,0},{3,1},{4,6},{5,7},{6,4},{7,5},{8,10},{9,11},{10,... | collective-permute-start | bytes 786440 | tf_op jit(solution)/shard_map/ppermute | solution.py:441
  118.7 20.8 %collective-permute-start.6 = (f32[16,32,128]{2,1,0:T(8,128)}, f32[16,32,128]{2,1,0:T(8,128)S(1)}, u32[]{:S(2)}, u32[]{:S(2)}) collective-permute-start(f32[16,32,128]{2,1,0:T(8,128)} %get-tuple-element.39), channel_id=1, source_target_pairs={{0,3},{1,0},{2,1},{3,2},{4,7},{5,4},{6,5},{7,6},{8,11},{9,8},{10,9... | collective-permute-start | bytes 786440 | tf_op jit(solution)/shard_map/ppermute | solution.py:441
  135.7 12.6 %collective-permute-start.21 = (f32[16,32,128]{2,1,0:T(8,128)S(1)}, f32[16,32,128]{2,1,0:T(8,128)S(1)}, u32[]{:S(2)}, u32[]{:S(2)}) collective-permute-start(f32[16,32,128]{2,1,0:T(8,128)S(1)} %get-tuple-element.58), channel_id=1, source_target_pairs={{0,8},{4,12},{8,16},{12,20},{16,24},{20,28},{24,0},{28,4},{1,9},{5... | collective-permute-start | bytes 786440 | tf_op jit(solution)/shard_map/ppermute | solution.py:441
  137.0 46.3 %collective-permute-start.22 = (f32[16,32,128]{2,1,0:T(8,128)S(1)}, f32[16,32,128]{2,1,0:T(8,128)S(1)}, u32[]{:S(2)}, u32[]{:S(2)}) collective-permute-start(f32[16,32,128]{2,1,0:T(8,128)S(1)} %get-tuple-element.59), channel_id=1, source_target_pairs={{0,12},{4,16},{8,20},{12,24},{16,28},{20,0},{24,4},{28,8},{1,13},{... | collective-permute-start | bytes 786440 | tf_op jit(solution)/shard_map/ppermute | solution.py:441
  139.3 49.6 %collective-permute-start.23 = (f32[16,32,128]{2,1,0:T(8,128)S(1)}, f32[16,32,128]{2,1,0:T(8,128)S(1)}, u32[]{:S(2)}, u32[]{:S(2)}) collective-permute-start(f32[16,32,128]{2,1,0:T(8,128)S(1)} %get-tuple-element.60), channel_id=1, source_target_pairs={{0,16},{4,20},{8,24},{12,28},{16,0},{20,4},{24,8},{28,12},{1,17},{... | collective-permute-start | bytes 786440 | tf_op jit(solution)/shard_map/ppermute | solution.py:441
  139.5 49.5 %collective-permute-start.24 = (f32[16,32,128]{2,1,0:T(8,128)S(1)}, f32[16,32,128]{2,1,0:T(8,128)S(1)}, u32[]{:S(2)}, u32[]{:S(2)}) collective-permute-start(f32[16,32,128]{2,1,0:T(8,128)S(1)} %get-tuple-element.61), channel_id=1, source_target_pairs={{0,20},{4,24},{8,28},{12,0},{16,4},{20,8},{24,12},{28,16},{1,21},{... | collective-permute-start | bytes 786440 | tf_op jit(solution)/shard_map/ppermute | solution.py:441
  141.4 47.8 %collective-permute-start.25 = (f32[16,32,128]{2,1,0:T(8,128)S(1)}, f32[16,32,128]{2,1,0:T(8,128)S(1)}, u32[]{:S(2)}, u32[]{:S(2)}) collective-permute-start(f32[16,32,128]{2,1,0:T(8,128)S(1)} %get-tuple-element.62), channel_id=1, source_target_pairs={{0,24},{4,28},{8,0},{12,4},{16,8},{20,12},{24,16},{28,20},{1,25},{... | collective-permute-start | bytes 786440 | tf_op jit(solution)/shard_map/ppermute | solution.py:441
  148.3 40.9 %collective-permute-start.26 = (f32[16,32,128]{2,1,0:T(8,128)S(1)}, f32[16,32,128]{2,1,0:T(8,128)S(1)}, u32[]{:S(2)}, u32[]{:S(2)}) collective-permute-start(f32[16,32,128]{2,1,0:T(8,128)S(1)} %get-tuple-element.63), channel_id=1, source_target_pairs={{0,28},{4,0},{8,4},{12,8},{16,12},{20,16},{24,20},{28,24},{1,29},{... | collective-permute-start | bytes 786440 | tf_op jit(solution)/shard_map/ppermute | solution.py:441
  183.3 19.7 %collective-permute-start.10 = (f32[16,32,128]{2,1,0:T(8,128)S(1)}, f32[16,32,128]{2,1,0:T(8,128)S(1)}, u32[]{:S(2)}, u32[]{:S(2)}) collective-permute-start(f32[16,32,128]{2,1,0:T(8,128)S(1)} %get-tuple-element.44), channel_id=1, source_target_pairs={{0,16},{4,20},{8,24},{12,28},{16,0},{20,4},{24,8},{28,12},{1,17},{... | collective-permute-start | bytes 786440 | tf_op jit(solution)/shard_map/ppermute | solution.py:441
  188.9 14.1 %collective-permute-start.11 = (f32[16,32,128]{2,1,0:T(8,128)S(1)}, f32[16,32,128]{2,1,0:T(8,128)S(1)}, u32[]{:S(2)}, u32[]{:S(2)}) collective-permute-start(f32[16,32,128]{2,1,0:T(8,128)S(1)} %get-tuple-element.45), channel_id=1, source_target_pairs={{0,20},{4,24},{8,28},{12,0},{16,4},{20,8},{24,12},{28,16},{1,21},{... | collective-permute-start | bytes 786440 | tf_op jit(solution)/shard_map/ppermute | solution.py:441
  189.0 32.2 %collective-permute-start.12 = (f32[16,32,128]{2,1,0:T(8,128)S(1)}, f32[16,32,128]{2,1,0:T(8,128)S(1)}, u32[]{:S(2)}, u32[]{:S(2)}) collective-permute-start(f32[16,32,128]{2,1,0:T(8,128)S(1)} %get-tuple-element.46), channel_id=1, source_target_pairs={{0,24},{4,28},{8,0},{12,4},{16,8},{20,12},{24,16},{28,20},{1,25},{... | collective-permute-start | bytes 786440 | tf_op jit(solution)/shard_map/ppermute | solution.py:441
  195.8 44.0 %collective-permute-start.27 = (f32[2,16,32,128]{3,2,1,0:T(8,128)S(1)}, f32[2,16,32,128]{3,2,1,0:T(8,128)S(1)}, u32[]{:S(2)}, u32[]{:S(2)}) collective-permute-start(f32[2,16,32,128]{3,2,1,0:T(8,128)S(1)} %get-tuple-element.65), channel_id=1, source_target_pairs={{0,1},{1,2},{2,3},{3,0},{4,5},{5,6},{6,7},{7,4},{8,9},{9,10},{10,1... | collective-permute-start | bytes 1572872 | tf_op jit(solution)/shard_map/ppermute | solution.py:441
  196.6 32.6 %collective-permute-start.13 = (f32[16,32,128]{2,1,0:T(8,128)S(1)}, f32[16,32,128]{2,1,0:T(8,128)S(1)}, u32[]{:S(2)}, u32[]{:S(2)}) collective-permute-start(f32[16,32,128]{2,1,0:T(8,128)S(1)} %get-tuple-element.47), channel_id=1, source_target_pairs={{0,28},{4,0},{8,4},{12,8},{16,12},{20,16},{24,20},{28,24},{1,29},{... | collective-permute-start | bytes 786440 | tf_op jit(solution)/shard_map/ppermute | solution.py:441
  203.0 26.3 %collective-permute-start.7 = (f32[16,32,128]{2,1,0:T(8,128)S(1)}, f32[16,32,128]{2,1,0:T(8,128)S(1)}, u32[]{:S(2)}, u32[]{:S(2)}) collective-permute-start(f32[16,32,128]{2,1,0:T(8,128)S(1)} %get-tuple-element.41), channel_id=1, source_target_pairs={{0,4},{4,8},{8,12},{12,16},{16,20},{20,24},{24,28},{28,0},{1,5},{5... | collective-permute-start | bytes 786440 | tf_op jit(solution)/shard_map/ppermute | solution.py:441
  203.0 27.2 %collective-permute-start.8 = (f32[16,32,128]{2,1,0:T(8,128)S(1)}, f32[16,32,128]{2,1,0:T(8,128)S(1)}, u32[]{:S(2)}, u32[]{:S(2)}) collective-permute-start(f32[16,32,128]{2,1,0:T(8,128)S(1)} %get-tuple-element.42), channel_id=1, source_target_pairs={{0,8},{4,12},{8,16},{12,20},{16,24},{20,28},{24,0},{28,4},{1,9},{5... | collective-permute-start | bytes 786440 | tf_op jit(solution)/shard_map/ppermute | solution.py:441
  229.2 19.6 %collective-permute-start.28 = (f32[2,16,32,128]{3,2,1,0:T(8,128)S(1)}, f32[2,16,32,128]{3,2,1,0:T(8,128)S(1)}, u32[]{:S(2)}, u32[]{:S(2)}) collective-permute-start(f32[2,16,32,128]{3,2,1,0:T(8,128)S(1)} %get-tuple-element.66), channel_id=1, source_target_pairs={{0,2},{1,3},{2,0},{3,1},{4,6},{5,7},{6,4},{7,5},{8,10},{9,11},{10,... | collective-permute-start | bytes 1572872 | tf_op jit(solution)/shard_map/ppermute | solution.py:441
  229.2 19.5 %collective-permute-start.29 = (f32[2,16,32,128]{3,2,1,0:T(8,128)S(1)}, f32[2,16,32,128]{3,2,1,0:T(8,128)S(1)}, u32[]{:S(2)}, u32[]{:S(2)}) collective-permute-start(f32[2,16,32,128]{3,2,1,0:T(8,128)S(1)} %get-tuple-element.67), channel_id=1, source_target_pairs={{0,3},{1,0},{2,1},{3,2},{4,7},{5,4},{6,5},{7,6},{8,11},{9,8},{10,9... | collective-permute-start | bytes 1572872 | tf_op jit(solution)/shard_map/ppermute | solution.py:441
  236.9 13.7 %collective-permute-start.14 = (f32[2,16,32,128]{3,2,1,0:T(8,128)S(1)}, f32[2,16,32,128]{3,2,1,0:T(8,128)S(1)}, u32[]{:S(2)}, u32[]{:S(2)}) collective-permute-start(f32[2,16,32,128]{3,2,1,0:T(8,128)S(1)} %get-tuple-element.49), channel_id=1, source_target_pairs={{0,1},{1,2},{2,3},{3,0},{4,5},{5,6},{6,7},{7,4},{8,9},{9,10},{10,1... | collective-permute-start | bytes 1572872 | tf_op jit(solution)/shard_map/ppermute | solution.py:441
  238.4 31.1 %collective-permute-start.15 = (f32[2,16,32,128]{3,2,1,0:T(8,128)S(1)}, f32[2,16,32,128]{3,2,1,0:T(8,128)S(1)}, u32[]{:S(2)}, u32[]{:S(2)}) collective-permute-start(f32[2,16,32,128]{3,2,1,0:T(8,128)S(1)} %get-tuple-element.50), channel_id=1, source_target_pairs={{0,2},{1,3},{2,0},{3,1},{4,6},{5,7},{6,4},{7,5},{8,10},{9,11},{10,... | collective-permute-start | bytes 1572872 | tf_op jit(solution)/shard_map/ppermute | solution.py:441
  239.8 29.6 %collective-permute-start.16 = (f32[2,16,32,128]{3,2,1,0:T(8,128)S(1)}, f32[2,16,32,128]{3,2,1,0:T(8,128)S(1)}, u32[]{:S(2)}, u32[]{:S(2)}) collective-permute-start(f32[2,16,32,128]{3,2,1,0:T(8,128)S(1)} %get-tuple-element.51), channel_id=1, source_target_pairs={{0,3},{1,0},{2,1},{3,2},{4,7},{5,4},{6,5},{7,6},{8,11},{9,8},{10,9... | collective-permute-start | bytes 1572872 | tf_op jit(solution)/shard_map/ppermute | solution.py:441
  (19 other events, 568.0 us)
where the time goes:
time: 281 us
  waiting for transfers between devices  120 us (43%)
  Pallas kernels  103 us (37%)
  starting transfers between devices  36.9 us (13%)
  blocking collectives  10.5 us (4%)
  local copies, waits for them, and re-layouts  7.11 us (3%)
    ppermute x26, waiting for transfers between devices, exchange(): lax.ppermute(blocks[s], axis, [(i, (i + s) % count) for i in range(count)])  99 us
    pallas_call x1, Pallas kernels, body(): pl.pallas_call(functools.partial(source_kernel, g), out_shape=[shape(T, Z...  36.8 us
    ppermute x26, starting transfers between devices, exchange(): lax.ppermute(blocks[s], axis, [(i, (i + s) % count) for i in range(count)])  32.5 us
    pallas_call x1, Pallas kernels, body(): pl.pallas_call(functools.partial(sums_kernel, g), out_shape=shape(8, R),...  31.3 us
    pallas_call x2, Pallas kernels, body(): pl.pallas_call(functools.partial(turn_kernel, g), out_shape=[shape(2, rb,...  13.3 us
    pallas_call x1, Pallas kernels, body(): pl.pallas_call(functools.partial(solve_kernel, g), out_shape=shape(2, mb,...  11.2 us
    ppermute x2, waiting for transfers between devices, pair(): lax.ppermute(low, axis, backward)  10.8 us
    pallas_call x2, Pallas kernels, body(): pl.pallas_call(functools.partial(axial_kernel, g), out_shape=[shape(rb, k...  10.6 us
  transfers between devices with their start and end apart: 30, of which 15 were waited for; matrix products, arithmetic and copies ran while one was open for 2% of the time, Pallas kernels for 9%

commit v1 on v0

--- a/solution.py
+++ b/solution.py
@@ -14,7 +14,9 @@
 time_step = 2.0
 filter_ratio = 4.0
 epsilon_den = 1e-06
-CHUNKS = 2
+CHUNK_EDGES = (0, 6, 16, 26, 32)
+UNROLL_SUMS = 1
+UNROLL = 4
 VMEM_BYTES = 60 * 1024 * 1024
 ANY = pl.BlockSpec(memory_space=pl.ANY)
 VM = pl.BlockSpec(memory_space=pltpu.VMEM)
@@ -26,6 +28,21 @@
 
 def round_up(value, unit):
     return (value + unit - 1) // unit * unit
+
+
+def odd_tiles(rows):
+    return (round_up(rows, 8) // 8 | 1) * 8
+
+
+def loop(count, most, step):
+    unit = next(u for u in range(most, 0, -1) if count % u == 0)
+
+    def several(i, carry):
+        for slot in range(unit):
+            step(i * unit + slot, slot)
+        return carry
+
+    lax.fori_loop(0, count // unit, several, 0)
 
 
 class Grid:
@@ -33,15 +50,15 @@
         self.nt = lax.axis_size("theta")
         self.ng = lax.axis_size("gz")
         _, self.T, self.Z, self.R = velocity.shape
+        self.chunks = len(CHUNK_EDGES) - 1
         self.NTH = self.T * self.nt
         self.NZ = self.Z * self.ng
         self.kb = self.NZ // self.nt
         self.mb = self.NTH // self.ng
-        self.chunks = CHUNKS
-        while self.R % (self.chunks * self.ng):
-            self.chunks //= 2
-        self.rc = self.R // self.chunks
-        self.rb = self.rc // self.ng
+        share = self.R // self.ng
+        edges = [round(share * e / 32.0 / 2) * 2 for e in CHUNK_EDGES]
+        self.first = edges[:-1]
+        self.rb = [b - a for a, b in zip(edges, edges[1:])]
         self.kz = 0.5 * self.NZ / pipe_length
         self.kt = 0.5 * self.NTH / (2.0 * math.pi)
 
@@ -106,12 +123,13 @@
     ]
     for copy in copies:
         copy.start()
-    rows = pad.reshape(3 * (T + 6) * (Z + 16), g.R)
+    pitch = pad.shape[2]
+    rows = pad.reshape(3 * (T + 6) * pitch, g.R)
     for c in range(3):
         for i in range(3):
-            first = c * (T + 6) * (Z + 16)
-            rows[pl.ds(first + 5 + i, T + 6, stride=Z + 16), :] = zlo[c, i]
-            rows[pl.ds(first + 8 + Z + i, T + 6, stride=Z + 16), :] = zhi[c, i]
+            first = c * (T + 6) * pitch
+            rows[pl.ds(first + 5 + i, T + 6, stride=pitch), :] = zlo[c, i]
+            rows[pl.ds(first + 8 + Z + i, T + 6, stride=pitch), :] = zhi[c, i]
     for copy in copies:
         copy.wait()
 
@@ -125,16 +143,16 @@
     rows = (inverse, up, down, g.kt * inverse)
     acc[...] = jnp.zeros_like(acc)
 
-    def step(t, carry):
-        for zc in range(raw.shape[1] // 8):
+    def step(t, slot):
+        for zc in range(round_up(g.Z + 2, 8) // 8):
             z = 7 + 8 * zc
             u, s = strain_rows(pad, t + 2, z, g, rows)
             size = size_of(s)
             here = pl.ds(8 * zc, 8)
             for n, (a, b) in enumerate(PAIRS):
-                raw[n, here, :] = u[a] * u[b]
-                raw[6 + n, here, :] = s[n]
-                raw[12 + n, here, :] = size * s[n]
+                raw[slot, n, here, :] = u[a] * u[b]
+                raw[slot, 6 + n, here, :] = s[n]
+                raw[slot, 12 + n, here, :] = size * s[n]
         live = t >= 2
 
         def smooth(n, load, zc):
@@ -153,7 +171,7 @@
                 for c in range(3)
             ]
             field = lambda n: smooth(
-                3 + n, lambda d: raw[n, 8 * zc + d : 8 * zc + d + 8, :], zc
+                3 + n, lambda d: raw[slot, n, 8 * zc + d : 8 * zc + d + 8, :], zc
             )
             scaled = [m * 0.0625 for m in mean]
             leonard = [field(n) - scaled[a] * mean[b] for n, (a, b) in enumerate(PAIRS)]
@@ -167,9 +185,8 @@
             side = model[3] * model[3] + model[4] * model[4] + model[5] * model[5]
             acc[0] += jnp.where(live, numer, 0.0)
             acc[1] += jnp.where(live, diag + 0.5 * side, 0.0)
-        return carry
-
-    lax.fori_loop(0, g.T + 2, step, 0)
+
+    loop(g.T + 2, UNROLL_SUMS, step)
     w = width[...] * (2.0 / 16.0)
     numer = jnp.sum(acc[0], axis=0, keepdims=True) * (w[:1] * (1.0 / 16.0))
     denom = jnp.sum(acc[1], axis=0, keepdims=True) * (w[:1] * w[:1])
@@ -189,7 +206,7 @@
     coefficient = total[0:1] / (total[1:2] + epsilon_den)
     strength = jnp.broadcast_to(coefficient, (8, R)) * width[...]
 
-    def stress_row(t, carry):
+    def stress_row(t, slot):
         for zc in range(eddy.shape[1] // 8):
             z = 6 + 8 * zc
             _, s = strain_rows(pad, t + 1, z, g, rows)
@@ -201,9 +218,8 @@
             for n in range(3):
                 tau[n, t, here, :] = main * s[n]
                 tau[3 + n, t, here, :] = side * s[3 + n]
-        return carry
-
-    lax.fori_loop(0, T + 4, stress_row, 0)
+
+    loop(T + 4, UNROLL, stress_row)
 
     def slab(n, t, z):
         return tau[n, t, z : z + 8, :]
@@ -211,7 +227,7 @@
     def radial(f):
         return shift_up(f) * up - shift_down(f) * down
 
-    def turn_row(a, carry):
+    def turn_row(a, slot):
         t = a + 1
         for zc in range(Z // 8):
             z = 2 + 8 * zc
@@ -223,15 +239,14 @@
                 + rt * (inverse + inverse)
             )
             vt[a, pl.ds(8 * zc, 8), :] = pad[1, a + 2, 8 + 8 * zc : 16 + 8 * zc, :] + force
-        return carry
-
-    lax.fori_loop(0, T + 2, turn_row, 0)
+
+    loop(T + 2, UNROLL, turn_row)
     r_up = shift_up(radius) * inverse * up
     r_down = shift_down(radius) * inverse * down
 
-    def source_row(a, carry):
+    def axial_row(a, slot):
         t = a + 2
-        for zc in range(vz.shape[0] // 8):
+        for zc in range(vz.shape[1] // 8):
             z = 1 + 8 * zc
             rz = slab(4, t, z)
             force = (
@@ -240,10 +255,14 @@
                 + (slab(2, t, z + 1) - slab(2, t, z - 1)) * g.kz
                 + rz * inverse
             )
-            vz[pl.ds(8 * zc, 8), :] = pad[2, a + 3, 7 + 8 * zc : 15 + 8 * zc, :] + force
+            vz[a, pl.ds(8 * zc, 8), :] = pad[2, a + 3, 7 + 8 * zc : 15 + 8 * zc, :] + force
+
+    loop(T, UNROLL, axial_row)
+
+    def radial_row(a, slot):
+        t = a + 2
         for zc in range(Z // 8):
             z = 2 + 8 * zc
-            here = pl.ds(8 * zc, 8)
             rr = slab(0, t, z)
             force = (
                 radial(rr)
@@ -251,36 +270,41 @@
                 + (slab(4, t, z + 1) - slab(4, t, z - 1)) * g.kz
                 + (rr - slab(1, t, z)) * inverse
             )
-            vr = pad[0, a + 3, 8 + 8 * zc : 16 + 8 * zc, :] + force
+            src[a, pl.ds(8 * zc, 8), :] = pad[0, a + 3, 8 + 8 * zc : 16 + 8 * zc, :] + force
+            ratio[a, pl.ds(8 * zc, 8), :] = eddy[t, z : z + 8, :]
+
+    loop(T, UNROLL, radial_row)
+
+    def source_row(a, slot):
+        for zc in range(Z // 8):
+            here = pl.ds(8 * zc, 8)
+            vr = src[a, here, :]
             src[a, here, :] = (
                 shift_up(vr) * r_up
                 - shift_down(vr) * r_down
                 + (vt[a + 2, here, :] - vt[a, here, :]) * kt
-                + (vz[8 * zc + 2 : 8 * zc + 10, :] - vz[8 * zc : 8 * zc + 8, :]) * g.kz
+                + (vz[a, 8 * zc + 2 : 8 * zc + 10, :] - vz[a, 8 * zc : 8 * zc + 8, :]) * g.kz
             )
-            ratio[a, here, :] = eddy[t, z : z + 8, :]
-        return carry
-
-    lax.fori_loop(0, T, source_row, 0)
+
+    loop(T, UNROLL, source_row)
     flat = src.reshape(T * src.shape[1], R)
     turned = flip.reshape(R * flip.shape[1], 2 * T)
 
-    def flip_step(p, carry):
+    def flip_step(p, slot):
         even = flat[pl.ds(2 * p, T, stride=src.shape[1]), :]
         odd = flat[pl.ds(2 * p + 1, T, stride=src.shape[1]), :]
         turned[pl.ds(p, R, stride=flip.shape[1]), :] = jnp.concatenate([even, odd], axis=0).T
-        return carry
-
-    lax.fori_loop(0, Z // 2, flip_step, 0)
+
+    loop(Z // 2, UNROLL, flip_step)
     me = lax.axis_index("gz")
     copies = []
     for c in range(g.chunks):
         for s in range(g.ng):
-            first = c * g.rc + lax.rem(me + s, g.ng) * g.rb
+            first = g.ng * g.first[c] + lax.rem(me + s, g.ng) * g.rb[c]
             n = c * g.ng + s
             copies.append(
                 pltpu.make_async_copy(
-                    flip.at[pl.ds(first, g.rb), pl.ds(0, Z // 2), :], outs[n], osems.at[n]
+                    flip.at[pl.ds(first, g.rb[c]), pl.ds(0, Z // 2), :], outs[n], osems.at[n]
                 )
             )
     for copy in copies:
@@ -312,7 +336,7 @@
     return dot(a[0], b[0]) + (dot(a[1], b[0]) + dot(a[0], b[1]) + small)
 
 
-def axial_kernel(g, *refs):
+def axial_kernel(g, rb, *refs):
     blocks, tables = refs[: g.ng], refs[g.ng : g.ng + 3]
     outs = refs[g.ng + 3 : g.ng + 3 + g.nt]
     left = refs[g.ng + 3 + g.nt :]
@@ -325,7 +349,7 @@
             here = (pl.ds(d * kb, kb), pl.ds(4 * zp * s, 4 * zp))
             for n in range(3):
                 left[n][here] = tables[n][source, target]
-    per = 2 if g.rb % 2 == 0 else 1
+    per = 2 if rb % 2 == 0 else 1
     first = lax.broadcasted_iota(jnp.int32, (zp, 2 * T), 1) < T
 
     def column(r):
@@ -346,14 +370,14 @@
                 outs[d][per * i + q] = result[d * kb : (d + 1) * kb, q * 2 * T : (q + 1) * 2 * T]
         return carry
 
-    lax.fori_loop(0, g.rb // per, step, 0)
-
-
-def turn_kernel(g, *refs):
+    lax.fori_loop(0, rb // per, step, 0)
+
+
+def turn_kernel(g, rb, *refs):
     blocks, tables = refs[: g.nt], refs[g.nt : g.nt + 3]
     outs = refs[g.nt + 3 : g.nt + 3 + g.ng]
     mine, other = lax.axis_index("theta"), lax.axis_index("gz")
-    rows = g.rb * g.kb
+    rows = rb * g.kb
     left = split(jnp.concatenate([b[...].reshape(rows, 2 * g.T) for b in blocks], axis=1))
     for d in range(g.ng):
         target = lax.rem(other + d, g.ng)
@@ -362,7 +386,7 @@
         result = dot6(left, right)
         for c in range(2):
             part = result[:, c * g.mb : (c + 1) * g.mb]
-            outs[d][c] = part.reshape(g.rb, g.kb, g.mb)
+            outs[d][c] = part.reshape(rb, g.kb, g.mb)
 
 
 def solve_kernel(g, *refs):
@@ -374,11 +398,11 @@
     copies = []
     for c in range(g.chunks):
         for s in range(g.ng):
-            first = c * g.rc + lax.rem(mine + g.ng - s, g.ng) * g.rb
+            first = g.ng * g.first[c] + lax.rem(mine + g.ng - s, g.ng) * g.rb[c]
             n = c * g.ng + s
             copies.append(
                 pltpu.make_async_copy(
-                    blocks[n], data.at[:, pl.ds(first, g.rb), pl.ds(0, kb), :], sems.at[n]
+                    blocks[n], data.at[:, pl.ds(first, g.rb[c]), pl.ds(0, kb), :], sems.at[n]
                 )
             )
     for copy in copies:
@@ -404,7 +428,7 @@
         data[1, r, :kb, :] = im
         return cp, re, im
 
-    lax.fori_loop(0, R, forward, (zero, zero, zero), unroll=2)
+    lax.fori_loop(0, R, forward, (zero, zero, zero), unroll=4)
 
     def backward(i, carry):
         re, im = carry
@@ -416,18 +440,17 @@
         data[1, r, :kb, :] = im
         return re, im
 
-    lax.fori_loop(0, R, backward, (zero, zero), unroll=2)
+    lax.fori_loop(0, R, backward, (zero, zero), unroll=4)
     flat = data.reshape(2 * R * data.shape[2], mb)
     turned = flip.reshape(2 * mb * flip.shape[2], R)
     stores = []
     for c in range(2):
 
-        def flip_step(i, carry):
+        def flip_step(i, slot, c=c):
             rows = flat[pl.ds(c * R * data.shape[2] + i, R, stride=data.shape[2]), :]
             turned[pl.ds(c * mb * flip.shape[2] + i, mb, stride=flip.shape[2]), :] = rows.T
-            return carry
-
-        lax.fori_loop(0, kb, flip_step, 0)
+
+        loop(kb, UNROLL, flip_step)
         copy = pltpu.make_async_copy(flip.at[c, :, pl.ds(0, kb), :], out.at[c], osems.at[c])
         copy.start()
         stores.append(copy)
@@ -437,10 +460,16 @@
 
 def exchange(blocks, axis):
     count = len(blocks)
-    return [blocks[0]] + [
-        lax.ppermute(blocks[s], axis, [(i, (i + s) % count) for i in range(count)])
-        for s in range(1, count)
-    ]
+    received = [blocks[0]]
+    for s in range(1, count):
+        ring = [(i, (i + s) % count) for i in range(count)]
+        received.append(lax.ppermute(blocks[s], axis, ring))
+    return received
+
+
+def after(later, earlier):
+    joined = lax.optimization_barrier((list(later), list(earlier)))
+    return joined[0], joined[1]
 
 
 def halo(g, v):
@@ -497,15 +526,18 @@
 
 
 def body(velocity):
-    g = Grid(velocity)
-    T, Z, R, rb, kb, mb = g.T, g.Z, g.R, g.rb, g.kb, g.mb
+    return program(Grid(velocity), velocity)
+
+
+def program(g, velocity):
+    T, Z, R, kb, mb = g.T, g.Z, g.R, g.kb, g.mb
     f32 = jnp.float32
     shape = lambda *s: jax.ShapeDtypeStruct(s, f32)
     buf = lambda *s: pltpu.VMEM(s, f32)
     dma = pltpu.SemaphoreType.DMA
     edges = halo(g, velocity)
     width = width_row(g)
-    pad = buf(3, T + 6, Z + 16, R)
+    pad = buf(3, T + 6, odd_tiles(Z + 16), R)
     halo_specs = [ANY, ANY, ANY, VM, VM, VM]
     part = pl.pallas_call(
         functools.partial(sums_kernel, g),
@@ -514,9 +546,9 @@
         out_specs=VM,
         scratch_shapes=[
             pad,
-            buf(18, round_up(Z + 2, 8), R),
-            buf(21, Z, R),
-            buf(21, Z, R),
+            buf(UNROLL_SUMS, 18, odd_tiles(Z + 2), R),
+            buf(21, odd_tiles(Z), R),
+            buf(21, odd_tiles(Z), R),
             buf(2, 8, R),
             dma((3,)),
         ],
@@ -529,15 +561,16 @@
     )
     outs = pl.pallas_call(
         functools.partial(source_kernel, g),
-        out_shape=[shape(T, Z, R)] + [shape(rb, Z // 2, 2 * T)] * (g.chunks * g.ng),
+        out_shape=[shape(T, Z, R)]
+        + [shape(rb, Z // 2, 2 * T) for rb in g.rb for _ in range(g.ng)],
         in_specs=halo_specs + [VM],
         out_specs=[VM] + [ANY] * (g.chunks * g.ng),
         scratch_shapes=[
             pad,
-            buf(6, T + 4, round_up(Z + 4, 8) + 8, R),
+            buf(6, T + 5, odd_tiles(Z + 10), R),
             buf(T + 4, round_up(Z + 4, 8), R),
-            buf(T + 2, Z, R),
-            buf(round_up(Z + 2, 8), R),
+            buf(T + 2, odd_tiles(Z), R),
+            buf(T, round_up(Z + 2, 8), R),
             buf(T, Z + 8, R),
             buf(R, Z // 2 + 8, 2 * T),
             dma((3,)),
@@ -549,27 +582,32 @@
     ratio, pieces = outs[0], outs[1:]
     axial_tables = axial_table(g)
     turn_tables = turn_table(g)
-    modes = []
-    for c in range(g.chunks):
-        lines = exchange(pieces[c * g.ng : (c + 1) * g.ng], "gz")
+    axials, modes = [], []
+    for c, rb in enumerate(g.rb):
+        piece = pieces[c * g.ng : (c + 1) * g.ng]
+        if c >= 1:
+            piece, axials[c - 1] = after(piece, axials[c - 1])
+        line = exchange(piece, "gz")
         axial = pl.pallas_call(
-            functools.partial(axial_kernel, g),
+            functools.partial(axial_kernel, g, rb),
             out_shape=[shape(rb, kb, 2 * T)] * g.nt,
             in_specs=[VM] * (g.ng + 3),
             out_specs=[VM] * g.nt,
             scratch_shapes=[pltpu.VMEM((g.NZ, 2 * g.NZ), jnp.bfloat16)] * 3,
             compiler_params=params(24 * 1024 * 1024),
             name="axial_modes",
-        )(*lines, *axial_tables)
-        cycles = exchange(axial, "theta")
+        )(*line, *axial_tables)
+        axials.append(axial)
+    for c, rb in enumerate(g.rb):
+        cycle = exchange(axials[c], "theta")
         turned = pl.pallas_call(
-            functools.partial(turn_kernel, g),
+            functools.partial(turn_kernel, g, rb),
             out_shape=[shape(2, rb, kb, mb)] * g.ng,
             in_specs=[VM] * (g.nt + 3),
             out_specs=[VM] * g.ng,
             compiler_params=params(40 * 1024 * 1024),
             name="turn_modes",
-        )(*cycles, *turn_tables)
+        )(*cycle, *turn_tables)
         modes += exchange(turned, "gz")
     pressure = pl.pallas_call(
         functools.partial(solve_kernel, g),

time: 281 us -> 269 us (0.957)
  the two profiles are of different devices: /device:TPU:15 before, /device:TPU:0 now
where the time goes in v1:
time: 269 us
  starting transfers between devices  87.9 us (33%)
  Pallas kernels  83.7 us (31%)
  waiting for transfers between devices  71.4 us (27%)
  blocking collectives  15.5 us (6%)
  local copies, waits for them, and re-layouts  7.04 us (3%)
    ppermute x52, starting transfers between devices, exchange(): received.append(lax.ppermute(blocks[s], axis, ring))  80.2 us
    ppermute x52, waiting for transfers between devices, exchange(): received.append(lax.ppermute(blocks[s], axis, ring))  53.9 us
    pallas_call x1, Pallas kernels, program(): pl.pallas_call(functools.partial(sums_kernel, g), out_shape=shape(8, R),...  28.6 us
    pallas_call x1, Pallas kernels, program(): pl.pallas_call(functools.partial(source_kernel, g), out_shape=[shape(T, Z...  23.8 us
    all_to_all x1, blocking collectives, program(): lax.all_to_all(jnp.broadcast_to(part[None], (count, 8, R)), ('theta', 'gz...  15.5 us
    pallas_call x4, Pallas kernels, program(): pl.pallas_call(functools.partial(turn_kernel, g, rb), out_shape=[shape(2,...  13.7 us
    pallas_call x4, Pallas kernels, program(): pl.pallas_call(functools.partial(axial_kernel, g, rb), out_shape=[shape(r...  10.9 us
    ppermute x2, waiting for transfers between devices, pair(): lax.ppermute(low, axis, backward)  9.52 us
  transfers between devices with their start and end apart: 56, of which 20 were waited for; matrix products, arithmetic and copies ran while one was open for 2% of the time, Pallas kernels for 8%

profile of v1, /device:TPU:0, one launch (start us, length us, event | category | flops | bytes accessed | tf_op | source)
XLA Modules:
  0.0 268.5 jit_solution(8178308303408077940)
XLA Ops:
  2.0 4.6 %collective-permute-start.1 = (f32[3,3,64,128]{3,1,2,0:T(4,128)S(1)}, f32[3,3,64,128]{3,1,2,0:T(4,128)S(1)}, u32[]{:S(2)}, u32[]{:S(2)}) collective-permute-start(f32[3,3,64,128]{3,1,2,0:T(4,128)S(1)} %copy.19), channel_id=1, source_target_pairs={{4,0},{8,4},{12,8},{16,12},{20,16},{24,20},{28,24},{0,28},{5,1},{9... | collective-permute-start | bytes 884744 | tf_op jit(solution)/shard_map/ppermute | solution.py:481
  8.4 5.9 %collective-permute-done.1 = f32[3,3,64,128]{3,1,2,0:T(4,128)S(1)} collective-permute-done((f32[3,3,64,128]{3,1,2,0:T(4,128)S(1)}, f32[3,3,64,128]{3,1,2,0:T(4,128)S(1)}, u32[]{:S(2)}, u32[]{:S(2)}) %collective-permute-start.1) | collective-permute-done | bytes 294944 | tf_op jit(solution)/shard_map/ppermute | solution.py:481
  21.6 5.2 %collective-permute-done.2.zlo = f32[3,3,70,128]{3,2,1,0:T(8,128)S(1)} collective-permute-done((f32[3,3,70,128]{3,2,1,0:T(8,128)S(1)}, f32[3,3,70,128]{3,2,1,0:T(8,128)S(1)}, u32[]{:S(2)}, u32[]{:S(2)}) %collective-permute-start.2) | collective-permute-done | bytes 322592 | tf_op jit(solution)/shard_map/ppermute | solution.py:481
  26.9 3.6 %collective-permute-done.3.zhi = f32[3,3,70,128]{3,2,1,0:T(8,128)S(1)} collective-permute-done((f32[3,3,70,128]{3,2,1,0:T(8,128)S(1)}, f32[3,3,70,128]{3,2,1,0:T(8,128)S(1)}, u32[]{:S(2)}, u32[]{:S(2)}) %collective-permute-start.3) | collective-permute-done | bytes 322592 | tf_op jit(solution)/shard_map/ppermute | solution.py:481
  31.2 28.6 %germano_sums.1 = f32[8,128]{1,0:T(8,128)} custom-call(f32[3,64,64,128]{3,2,1,0:T(8,128)} %v.3, f32[3,3,64,128]{3,2,1,0:T(8,128)} %copy.16.tlo, f32[3,3,64,128]{3,2,1,0:T(8,128)} %copy.17.thi, f32[3,3,70,128]{3,2,1,0:T(8,128)} %copy-done.8, f32[3,3,70,128]{3,2,1,0:T(8,128)} %copy-done.9, f32[8,128]{1,0:T(8,128)} %jit_solution_.3.width), custom_call_target="tpu_custom_call" | custom-call | tf_op jit(solution)/shard_map/germano_sums/pallas_call | solution.py:542
  60.6 15.5 %all_to_all.5.sums = f32[32,8,128]{2,1,0:T(8,128)} all-to-all(f32[32,8,128]{2,1,0:T(8,128)S(1)} %broadcast_in_dim.2), channel_id=1, replica_groups=mesh['theta'=8,'gz'=4] {'theta','gz'}, dimensions={0} | all-to-all | bytes 262144 | tf_op jit(solution)/shard_map/all_to_all | solution.py:559
  76.1 23.8 %source.1 = (f32[64,64,128]{2,1,0:T(8,128)}, f32[6,32,128]{2,1,0:T(8,128)}, f32[6,32,128]{2,1,0:T(8,128)}, f32[6,32,128]{2,1,0:T(8,128)}, f32[6,32,128]{2,1,0:T(...) custom-call(f32[3,64,64,128]{3,2,1,0:T(8,128)} %v.3, ...), custom_call_target="tpu_custom_call" | custom-call | tf_op jit(solution)/shard_map/source/pallas_call | solution.py:562
  103.2 3.1 %collective-permute-done.4.refs_1_ = f32[6,32,128]{2,1,0:T(8,128)S(1)} collective-permute-done((f32[6,32,128]{2,1,0:T(8,128)}, f32[6,32,128]{2,1,0:T(8,128)S(1)}, u32[]{:S(2)}, u32[]{:S(2)}) %collective-permute-start.4) | collective-permute-done | bytes 98336 | tf_op jit(solution)/shard_map/ppermute | solution.py:466
  118.3 7.0 %collective-permute-done.9.refs_3_ = f32[6,32,128]{2,1,0:T(8,128)S(1)} collective-permute-done((f32[6,32,128]{2,1,0:T(8,128)S(1)}, f32[6,32,128]{2,1,0:T(8,128)S(1)}, u32[]{:S(2)}, u32[]{:S(2)}) %collective-permute-start.9) | collective-permute-done | bytes 98336 | tf_op jit(solution)/shard_map/ppermute | solution.py:466
  135.7 3.4 %axial_modes.5 = (f32[10,32,128]{2,1,0:T(8,128)S(1)}, f32[10,32,128]{2,1,0:T(8,128)S(1)}, f32[10,32,128]{2,1,0:T(8,128)S(1)}, f32[10,32,128]{2,1,0:T(8,128)S(1)}...) custom-call(f32[10,32,128]{2,1,0:T(8,128)S(1)} %copy-done.4, ...), custom_call_target="tpu_custom_call" | custom-call | tf_op jit(solution)/shard_map/axial_modes/pallas_call | solution.py:591
  144.8 4.2 %collective-permute-done.15.refs_2_ = f32[2,6,32,128]{3,2,1,0:T(8,128)S(1)} collective-permute-done((f32[2,6,32,128]{3,2,1,0:T(8,128)S(1)}, f32[2,6,32,128]{3,2,1,0:T(8,128)S(1)}, u32[]{:S(2)}, u32[]{:S(2)}) %collective-permute-start.15) | collective-permute-done | bytes 196640 | tf_op jit(solution)/shard_map/ppermute | solution.py:466
  152.5 3.6 %collective-permute-start.25 = (f32[10,32,128]{2,1,0:T(8,128)S(1)}, f32[10,32,128]{2,1,0:T(8,128)S(1)}, u32[]{:S(2)}, u32[]{:S(2)}) collective-permute-start(f32[10,32,128]{2,1,0:T(8,128)S(1)} %get-tuple-element.154), channel_id=1, source_target_pairs={{0,24},{4,28},{8,0},{12,4},{16,8},{20,12},{24,16},{28,20},{1,25},{... | collective-permute-start | bytes 491528 | tf_op jit(solution)/shard_map/ppermute | solution.py:466
  156.4 3.4 %axial_modes.6 = (f32[10,32,128]{2,1,0:T(8,128)S(1)}, f32[10,32,128]{2,1,0:T(8,128)S(1)}, f32[10,32,128]{2,1,0:T(8,128)S(1)}, f32[10,32,128]{2,1,0:T(8,128)S(1)}...) custom-call(f32[10,32,128]{2,1,0:T(8,128)S(1)} %copy-done.3, ...), custom_call_target="tpu_custom_call" | custom-call | tf_op jit(solution)/shard_map/axial_modes/pallas_call | solution.py:591
  171.9 4.2 %collective-permute-start.34 = (f32[10,32,128]{2,1,0:T(8,128)S(1)}, f32[10,32,128]{2,1,0:T(8,128)S(1)}, u32[]{:S(2)}, u32[]{:S(2)}) collective-permute-start(f32[10,32,128]{2,1,0:T(8,128)S(1)} %get-tuple-element.178), channel_id=1, source_target_pairs={{0,8},{4,12},{8,16},{12,20},{16,24},{20,28},{24,0},{28,4},{1,9},{5... | collective-permute-start | bytes 491528 | tf_op jit(solution)/shard_map/ppermute | solution.py:466
  185.8 11.2 %collective-permute-done.35.refs_3_ = f32[10,32,128]{2,1,0:T(8,128)S(1)} collective-permute-done((f32[10,32,128]{2,1,0:T(8,128)S(1)}, f32[10,32,128]{2,1,0:T(8,128)S(1)}, u32[]{:S(2)}, u32[]{:S(2)}) %collective-permute-start.35) | collective-permute-done | bytes 163872 | tf_op jit(solution)/shard_map/ppermute | solution.py:466
  197.2 4.7 %collective-permute-start.48 = (f32[6,32,128]{2,1,0:T(8,128)S(1)}, f32[6,32,128]{2,1,0:T(8,128)S(1)}, u32[]{:S(2)}, u32[]{:S(2)}) collective-permute-start(f32[6,32,128]{2,1,0:T(8,128)S(1)} %get-tuple-element.195), channel_id=1, source_target_pairs={{0,12},{4,16},{8,20},{12,24},{16,28},{20,0},{24,4},{28,8},{1,13},{... | collective-permute-start | bytes 294920 | tf_op jit(solution)/shard_map/ppermute | solution.py:466
  201.9 3.1 %collective-permute-start.49 = (f32[6,32,128]{2,1,0:T(8,128)S(1)}, f32[6,32,128]{2,1,0:T(8,128)S(1)}, u32[]{:S(2)}, u32[]{:S(2)}) collective-permute-start(f32[6,32,128]{2,1,0:T(8,128)S(1)} %get-tuple-element.196), channel_id=1, source_target_pairs={{0,16},{4,20},{8,24},{12,28},{16,0},{20,4},{24,8},{28,12},{1,17},{... | collective-permute-start | bytes 294920 | tf_op jit(solution)/shard_map/ppermute | solution.py:466
  205.0 7.4 %collective-permute-start.50 = (f32[6,32,128]{2,1,0:T(8,128)S(1)}, f32[6,32,128]{2,1,0:T(8,128)S(1)}, u32[]{:S(2)}, u32[]{:S(2)}) collective-permute-start(f32[6,32,128]{2,1,0:T(8,128)S(1)} %get-tuple-element.197), channel_id=1, source_target_pairs={{0,20},{4,24},{8,28},{12,0},{16,4},{20,8},{24,12},{28,16},{1,21},{... | collective-permute-start | bytes 294920 | tf_op jit(solution)/shard_map/ppermute | solution.py:466
  212.5 4.2 %turn_modes.5 = (f32[2,10,32,128]{3,2,1,0:T(8,128)S(1)}, f32[2,10,32,128]{3,2,1,0:T(8,128)S(1)}, f32[2,10,32,128]{3,2,1,0:T(8,128)S(1)}, f32[2,10,32,128]{3,2,1,0:T(8,128)S(1)}) custom-call(f32[10,32,128]{2,1,0:T(8,128)S(1)} %get-tuple-element.148.refs_0_, f32[10,32,128]{2,1,0:T(8,128)S(1)} %collective-permute-done.20.refs_1_, ...), custom_call_target="tpu_custom_call" | custom-call | tf_op jit(solution)/shard_map/turn_modes/pallas_call | solution.py:603
  218.2 3.4 %collective-permute-start.51 = (f32[6,32,128]{2,1,0:T(8,128)S(1)}, f32[6,32,128]{2,1,0:T(8,128)S(1)}, u32[]{:S(2)}, u32[]{:S(2)}) collective-permute-start(f32[6,32,128]{2,1,0:T(8,128)S(1)} %get-tuple-element.198), channel_id=1, source_target_pairs={{0,24},{4,28},{8,0},{12,4},{16,8},{20,12},{24,16},{28,20},{1,25},{... | collective-permute-start | bytes 294920 | tf_op jit(solution)/shard_map/ppermute | solution.py:466
  230.9 4.2 %turn_modes.6 = (f32[2,10,32,128]{3,2,1,0:T(8,128)S(1)}, f32[2,10,32,128]{3,2,1,0:T(8,128)S(1)}, f32[2,10,32,128]{3,2,1,0:T(8,128)S(1)}, f32[2,10,32,128]{3,2,1,0:T(8,128)S(1)}) custom-call(f32[10,32,128]{2,1,0:T(8,128)S(1)} %get-tuple-element.176.refs_0_, f32[10,32,128]{2,1,0:T(8,128)S(1)} %collective-permute-done.33.refs_1_, ...), custom_call_target="tpu_custom_call" | custom-call | tf_op jit(solution)/shard_map/turn_modes/pallas_call | solution.py:603
  237.6 3.6 %collective-permute-start.42 = (f32[2,10,32,128]{3,2,1,0:T(8,128)S(1)}, f32[2,10,32,128]{3,2,1,0:T(8,128)S(1)}, u32[]{:S(2)}, u32[]{:S(2)}) collective-permute-start(f32[2,10,32,128]{3,2,1,0:T(8,128)S(1)} %get-tuple-element.187), channel_id=1, source_target_pairs={{0,3},{1,0},{2,1},{3,2},{4,7},{5,4},{6,5},{7,6},{8,11},{9,8},{10,9... | collective-permute-start | bytes 983048 | tf_op jit(solution)/shard_map/ppermute | solution.py:466
  245.5 15.1 %collective-permute-done.54.refs_14_ = f32[2,6,32,128]{3,2,1,0:T(8,128)S(1)} collective-permute-done((f32[2,6,32,128]{3,2,1,0:T(8,128)S(1)}, f32[2,6,32,128]{3,2,1,0:T(8,128)S(1)}, u32[]{:S(2)}, u32[]{:S(2)}) %collective-permute-start.54) | collective-permute-done | bytes 196640 | tf_op jit(solution)/shard_map/ppermute | solution.py:466
  261.6 6.7 %solve_modes.1 = f32[2,128,32,128]{3,2,1,0:T(8,128)} custom-call(f32[2,6,32,128]{3,2,1,0:T(8,128)S(1)} %get-tuple-element.128.refs_0_, f32[2,6,32,128]{3,2,1,0:T(8,128)S(1)} %collective-permute-done.14.refs_1_, f32[2,6,32,128]{3,2,1,0:T(8,128)S(1)} %collective-permute-done.15.refs_2_, f32[2,6,32,128]{3,2,1,0:T(8,128)S(1)} %collective-permute-done.16.refs_3_, ...), custom_call_target="tpu_custom_call" | custom-call | tf_op jit(solution)/shard_map/solve_modes/pallas_call | solution.py:612
  (164 shorter events, 87.4 us)
Async XLA Ops:
  110.9 14.4 %collective-permute-start.9 = (f32[6,32,128]{2,1,0:T(8,128)S(1)}, f32[6,32,128]{2,1,0:T(8,128)S(1)}, u32[]{:S(2)}, u32[]{:S(2)}) collective-permute-start(f32[6,32,128]{2,1,0:T(8,128)S(1)} %get-tuple-element.123), channel_id=1, source_target_pairs={{0,12},{4,16},{8,20},{12,24},{16,28},{20,0},{24,4},{28,8},{1,13},{... | collective-permute-start | bytes 294920 | tf_op jit(solution)/shard_map/ppermute | solution.py:466
  112.1 15.4 %collective-permute-start.10 = (f32[6,32,128]{2,1,0:T(8,128)S(1)}, f32[6,32,128]{2,1,0:T(8,128)S(1)}, u32[]{:S(2)}, u32[]{:S(2)}) collective-permute-start(f32[6,32,128]{2,1,0:T(8,128)S(1)} %get-tuple-element.124), channel_id=1, source_target_pairs={{0,16},{4,20},{8,24},{12,28},{16,0},{20,4},{24,8},{28,12},{1,17},{... | collective-permute-start | bytes 294920 | tf_op jit(solution)/shard_map/ppermute | solution.py:466
  134.6 14.4 %collective-permute-start.15 = (f32[2,6,32,128]{3,2,1,0:T(8,128)S(1)}, f32[2,6,32,128]{3,2,1,0:T(8,128)S(1)}, u32[]{:S(2)}, u32[]{:S(2)}) collective-permute-start(f32[2,6,32,128]{3,2,1,0:T(8,128)S(1)} %get-tuple-element.130), channel_id=1, source_target_pairs={{0,2},{1,3},{2,0},{3,1},{4,6},{5,7},{6,4},{7,5},{8,10},{9,11},{10,... | collective-permute-start | bytes 589832 | tf_op jit(solution)/shard_map/ppermute | solution.py:466
  150.3 16.2 %collective-permute-start.23 = (f32[10,32,128]{2,1,0:T(8,128)S(1)}, f32[10,32,128]{2,1,0:T(8,128)S(1)}, u32[]{:S(2)}, u32[]{:S(2)}) collective-permute-start(f32[10,32,128]{2,1,0:T(8,128)S(1)} %get-tuple-element.152), channel_id=1, source_target_pairs={{0,16},{4,20},{8,24},{12,28},{16,0},{20,4},{24,8},{28,12},{1,17},{... | collective-permute-start | bytes 491528 | tf_op jit(solution)/shard_map/ppermute | solution.py:466
  151.9 15.6 %collective-permute-start.24 = (f32[10,32,128]{2,1,0:T(8,128)S(1)}, f32[10,32,128]{2,1,0:T(8,128)S(1)}, u32[]{:S(2)}, u32[]{:S(2)}) collective-permute-start(f32[10,32,128]{2,1,0:T(8,128)S(1)} %get-tuple-element.153), channel_id=1, source_target_pairs={{0,20},{4,24},{8,28},{12,0},{16,4},{20,8},{24,12},{28,16},{1,21},{... | collective-permute-start | bytes 491528 | tf_op jit(solution)/shard_map/ppermute | solution.py:466
  152.5 17.5 %collective-permute-start.25 = (f32[10,32,128]{2,1,0:T(8,128)S(1)}, f32[10,32,128]{2,1,0:T(8,128)S(1)}, u32[]{:S(2)}, u32[]{:S(2)}) collective-permute-start(f32[10,32,128]{2,1,0:T(8,128)S(1)} %get-tuple-element.154), channel_id=1, source_target_pairs={{0,24},{4,28},{8,0},{12,4},{16,8},{20,12},{24,16},{28,20},{1,25},{... | collective-permute-start | bytes 491528 | tf_op jit(solution)/shard_map/ppermute | solution.py:466
  156.1 15.8 %collective-permute-start.26 = (f32[10,32,128]{2,1,0:T(8,128)S(1)}, f32[10,32,128]{2,1,0:T(8,128)S(1)}, u32[]{:S(2)}, u32[]{:S(2)}) collective-permute-start(f32[10,32,128]{2,1,0:T(8,128)S(1)} %get-tuple-element.155), channel_id=1, source_target_pairs={{0,28},{4,0},{8,4},{12,8},{16,12},{20,16},{24,20},{28,24},{1,29},{... | collective-permute-start | bytes 491528 | tf_op jit(solution)/shard_map/ppermute | solution.py:466
  176.1 20.9 %collective-permute-start.35 = (f32[10,32,128]{2,1,0:T(8,128)S(1)}, f32[10,32,128]{2,1,0:T(8,128)S(1)}, u32[]{:S(2)}, u32[]{:S(2)}) collective-permute-start(f32[10,32,128]{2,1,0:T(8,128)S(1)} %get-tuple-element.179), channel_id=1, source_target_pairs={{0,12},{4,16},{8,20},{12,24},{16,28},{20,0},{24,4},{28,8},{1,13},{... | collective-permute-start | bytes 491528 | tf_op jit(solution)/shard_map/ppermute | solution.py:466
  177.1 20.1 %collective-permute-start.36 = (f32[10,32,128]{2,1,0:T(8,128)S(1)}, f32[10,32,128]{2,1,0:T(8,128)S(1)}, u32[]{:S(2)}, u32[]{:S(2)}) collective-permute-start(f32[10,32,128]{2,1,0:T(8,128)S(1)} %get-tuple-element.180), channel_id=1, source_target_pairs={{0,16},{4,20},{8,24},{12,28},{16,0},{20,4},{24,8},{28,12},{1,17},{... | collective-permute-start | bytes 491528 | tf_op jit(solution)/shard_map/ppermute | solution.py:466
  179.7 22.2 %collective-permute-start.37 = (f32[10,32,128]{2,1,0:T(8,128)S(1)}, f32[10,32,128]{2,1,0:T(8,128)S(1)}, u32[]{:S(2)}, u32[]{:S(2)}) collective-permute-start(f32[10,32,128]{2,1,0:T(8,128)S(1)} %get-tuple-element.181), channel_id=1, source_target_pairs={{0,20},{4,24},{8,28},{12,0},{16,4},{20,8},{24,12},{28,16},{1,21},{... | collective-permute-start | bytes 491528 | tf_op jit(solution)/shard_map/ppermute | solution.py:466
  182.4 22.7 %collective-permute-start.38 = (f32[10,32,128]{2,1,0:T(8,128)S(1)}, f32[10,32,128]{2,1,0:T(8,128)S(1)}, u32[]{:S(2)}, u32[]{:S(2)}) collective-permute-start(f32[10,32,128]{2,1,0:T(8,128)S(1)} %get-tuple-element.182), channel_id=1, source_target_pairs={{0,24},{4,28},{8,0},{12,4},{16,8},{20,12},{24,16},{28,20},{1,25},{... | collective-permute-start | bytes 491528 | tf_op jit(solution)/shard_map/ppermute | solution.py:466
  184.5 32.2 %collective-permute-start.46 = (f32[6,32,128]{2,1,0:T(8,128)S(1)}, f32[6,32,128]{2,1,0:T(8,128)S(1)}, u32[]{:S(2)}, u32[]{:S(2)}) collective-permute-start(f32[6,32,128]{2,1,0:T(8,128)S(1)} %get-tuple-element.193), channel_id=1, source_target_pairs={{0,4},{4,8},{8,12},{12,16},{16,20},{20,24},{24,28},{28,0},{1,5},{5... | collective-permute-start | bytes 294920 | tf_op jit(solution)/shard_map/ppermute | solution.py:466
  197.0 20.4 %collective-permute-start.47 = (f32[6,32,128]{2,1,0:T(8,128)S(1)}, f32[6,32,128]{2,1,0:T(8,128)S(1)}, u32[]{:S(2)}, u32[]{:S(2)}) collective-permute-start(f32[6,32,128]{2,1,0:T(8,128)S(1)} %get-tuple-element.194), channel_id=1, source_target_pairs={{0,8},{4,12},{8,16},{12,20},{16,24},{20,28},{24,0},{28,4},{1,9},{5... | collective-permute-start | bytes 294920 | tf_op jit(solution)/shard_map/ppermute | solution.py:466
  197.2 21.0 %collective-permute-start.48 = (f32[6,32,128]{2,1,0:T(8,128)S(1)}, f32[6,32,128]{2,1,0:T(8,128)S(1)}, u32[]{:S(2)}, u32[]{:S(2)}) collective-permute-start(f32[6,32,128]{2,1,0:T(8,128)S(1)} %get-tuple-element.195), channel_id=1, source_target_pairs={{0,12},{4,16},{8,20},{12,24},{16,28},{20,0},{24,4},{28,8},{1,13},{... | collective-permute-start | bytes 294920 | tf_op jit(solution)/shard_map/ppermute | solution.py:466
  201.9 19.6 %collective-permute-start.49 = (f32[6,32,128]{2,1,0:T(8,128)S(1)}, f32[6,32,128]{2,1,0:T(8,128)S(1)}, u32[]{:S(2)}, u32[]{:S(2)}) collective-permute-start(f32[6,32,128]{2,1,0:T(8,128)S(1)} %get-tuple-element.196), channel_id=1, source_target_pairs={{0,16},{4,20},{8,24},{12,28},{16,0},{20,4},{24,8},{28,12},{1,17},{... | collective-permute-start | bytes 294920 | tf_op jit(solution)/shard_map/ppermute | solution.py:466
  205.0 16.5 %collective-permute-start.50 = (f32[6,32,128]{2,1,0:T(8,128)S(1)}, f32[6,32,128]{2,1,0:T(8,128)S(1)}, u32[]{:S(2)}, u32[]{:S(2)}) collective-permute-start(f32[6,32,128]{2,1,0:T(8,128)S(1)} %get-tuple-element.197), channel_id=1, source_target_pairs={{0,20},{4,24},{8,28},{12,0},{16,4},{20,8},{24,12},{28,16},{1,21},{... | collective-permute-start | bytes 294920 | tf_op jit(solution)/shard_map/ppermute | solution.py:466
  216.7 19.7 %collective-permute-start.27 = (f32[2,10,32,128]{3,2,1,0:T(8,128)S(1)}, f32[2,10,32,128]{3,2,1,0:T(8,128)S(1)}, u32[]{:S(2)}, u32[]{:S(2)}) collective-permute-start(f32[2,10,32,128]{3,2,1,0:T(8,128)S(1)} %get-tuple-element.157), channel_id=1, source_target_pairs={{0,1},{1,2},{2,3},{3,0},{4,5},{5,6},{6,7},{7,4},{8,9},{9,10},{10,1... | collective-permute-start | bytes 983048 | tf_op jit(solution)/shard_map/ppermute | solution.py:466
  217.4 20.2 %collective-permute-start.28 = (f32[2,10,32,128]{3,2,1,0:T(8,128)S(1)}, f32[2,10,32,128]{3,2,1,0:T(8,128)S(1)}, u32[]{:S(2)}, u32[]{:S(2)}) collective-permute-start(f32[2,10,32,128]{3,2,1,0:T(8,128)S(1)} %get-tuple-element.158), channel_id=1, source_target_pairs={{0,2},{1,3},{2,0},{3,1},{4,6},{5,7},{6,4},{7,5},{8,10},{9,11},{10,... | collective-permute-start | bytes 983048 | tf_op jit(solution)/shard_map/ppermute | solution.py:466
  226.1 15.1 %collective-permute-start.29 = (f32[2,10,32,128]{3,2,1,0:T(8,128)S(1)}, f32[2,10,32,128]{3,2,1,0:T(8,128)S(1)}, u32[]{:S(2)}, u32[]{:S(2)}) collective-permute-start(f32[2,10,32,128]{3,2,1,0:T(8,128)S(1)} %get-tuple-element.159), channel_id=1, source_target_pairs={{0,3},{1,0},{2,1},{3,2},{4,7},{5,4},{6,5},{7,6},{8,11},{9,8},{10,9... | collective-permute-start | bytes 983048 | tf_op jit(solution)/shard_map/ppermute | solution.py:466
  235.1 26.5 %collective-permute-start.40 = (f32[2,10,32,128]{3,2,1,0:T(8,128)S(1)}, f32[2,10,32,128]{3,2,1,0:T(8,128)S(1)}, u32[]{:S(2)}, u32[]{:S(2)}) collective-permute-start(f32[2,10,32,128]{3,2,1,0:T(8,128)S(1)} %get-tuple-element.185), channel_id=1, source_target_pairs={{0,1},{1,2},{2,3},{3,0},{4,5},{5,6},{6,7},{7,4},{8,9},{9,10},{10,1... | collective-permute-start | bytes 983048 | tf_op jit(solution)/shard_map/ppermute | solution.py:466
  236.5 25.2 %collective-permute-start.41 = (f32[2,10,32,128]{3,2,1,0:T(8,128)S(1)}, f32[2,10,32,128]{3,2,1,0:T(8,128)S(1)}, u32[]{:S(2)}, u32[]{:S(2)}) collective-permute-start(f32[2,10,32,128]{3,2,1,0:T(8,128)S(1)} %get-tuple-element.186), channel_id=1, source_target_pairs={{0,2},{1,3},{2,0},{3,1},{4,6},{5,7},{6,4},{7,5},{8,10},{9,11},{10,... | collective-permute-start | bytes 983048 | tf_op jit(solution)/shard_map/ppermute | solution.py:466
  237.6 24.0 %collective-permute-start.42 = (f32[2,10,32,128]{3,2,1,0:T(8,128)S(1)}, f32[2,10,32,128]{3,2,1,0:T(8,128)S(1)}, u32[]{:S(2)}, u32[]{:S(2)}) collective-permute-start(f32[2,10,32,128]{3,2,1,0:T(8,128)S(1)} %get-tuple-element.187), channel_id=1, source_target_pairs={{0,3},{1,0},{2,1},{3,2},{4,7},{5,4},{6,5},{7,6},{8,11},{9,8},{10,9... | collective-permute-start | bytes 983048 | tf_op jit(solution)/shard_map/ppermute | solution.py:466
  241.2 19.4 %collective-permute-start.54 = (f32[2,6,32,128]{3,2,1,0:T(8,128)S(1)}, f32[2,6,32,128]{3,2,1,0:T(8,128)S(1)}, u32[]{:S(2)}, u32[]{:S(2)}) collective-permute-start(f32[2,6,32,128]{3,2,1,0:T(8,128)S(1)} %get-tuple-element.202), channel_id=1, source_target_pairs={{0,2},{1,3},{2,0},{3,1},{4,6},{5,7},{6,4},{7,5},{8,10},{9,11},{10,... | collective-permute-start | bytes 589832 | tf_op jit(solution)/shard_map/ppermute | solution.py:466
  243.8 17.8 %collective-permute-start.55 = (f32[2,6,32,128]{3,2,1,0:T(8,128)S(1)}, f32[2,6,32,128]{3,2,1,0:T(8,128)S(1)}, u32[]{:S(2)}, u32[]{:S(2)}) collective-permute-start(f32[2,6,32,128]{3,2,1,0:T(8,128)S(1)} %get-tuple-element.203), channel_id=1, source_target_pairs={{0,3},{1,0},{2,1},{3,2},{4,7},{5,4},{6,5},{7,6},{8,11},{9,8},{10,9... | collective-permute-start | bytes 589832 | tf_op jit(solution)/shard_map/ppermute | solution.py:466
  (56 other events, 972.5 us)

commit v2 on v1

--- a/solution.py
+++ b/solution.py
@@ -14,9 +14,10 @@
 time_step = 2.0
 filter_ratio = 4.0
 epsilon_den = 1e-06
-CHUNK_EDGES = (0, 6, 16, 26, 32)
-UNROLL_SUMS = 1
+CHUNK_EDGES = (0, 8, 16, 24, 32)
 UNROLL = 4
+SLOTS = 4
+PARTS = 4
 VMEM_BYTES = 60 * 1024 * 1024
 ANY = pl.BlockSpec(memory_space=pl.ANY)
 VM = pl.BlockSpec(memory_space=pltpu.VMEM)
@@ -34,10 +35,12 @@
     return (round_up(rows, 8) // 8 | 1) * 8
 
 
-def loop(count, most, step):
+def loop(count, most, step, before=None):
     unit = next(u for u in range(most, 0, -1) if count % u == 0)
 
     def several(i, carry):
+        if before is not None:
+            before(i, unit)
         for slot in range(unit):
             step(i * unit + slot, slot)
         return carry
@@ -86,9 +89,9 @@
     return pltpu.roll(f, 1, 1)
 
 
-def strain_rows(pad, t, z, g, rows):
+def strain_rows(fetch, t, z, g, rows):
     inverse, up, down, kt = rows
-    at = lambda c, dt, dz: pad[c, t + dt, z + dz : z + dz + 8, :]
+    at = lambda c, dt, dz: fetch(c, t + dt, z + dz)
     u = [at(c, 0, 0) for c in range(3)]
     radial = [shift_up(f) * up - shift_down(f) * down for f in u]
     turn = [(at(c, 1, 0) - at(c, -1, 0)) * kt for c in range(3)]
@@ -114,66 +117,73 @@
     return root((diag + diag) + (s[3] * s[3] + s[4] * s[4] + s[5] * s[5]))
 
 
-def fill_pad(g, v, tlo, thi, zlo, zhi, pad, sems):
+def put_columns(pad, block, row, z, values):
+    *_, height, pitch, R = pad.shape
+    flat = pad.reshape(math.prod(pad.shape[:-1]), R)
+    which = block[0] if len(block) == 1 else block[0] * 3 + block[1]
+    flat[pl.ds((which * height + row) * pitch + z, values.shape[0], stride=pitch), :] = values
+
+
+def fill_pad(g, v, edges, pad, sems):
     T, Z = g.T, g.Z
+    tlo, thi, zlo, zhi, *corners = edges
+    block = row_copies(v, pad, 3, sems)
     copies = [
-        pltpu.make_async_copy(v, pad.at[:, pl.ds(3, T), pl.ds(8, Z), :], sems.at[0]),
-        pltpu.make_async_copy(tlo, pad.at[:, pl.ds(0, 3), pl.ds(8, Z), :], sems.at[1]),
-        pltpu.make_async_copy(thi, pad.at[:, pl.ds(T + 3, 3), pl.ds(8, Z), :], sems.at[2]),
+        pltpu.make_async_copy(tlo, pad.at[:, pl.ds(0, 3), pl.ds(8, Z), :], sems.at[PARTS]),
+        pltpu.make_async_copy(thi, pad.at[:, pl.ds(T + 3, 3), pl.ds(8, Z), :], sems.at[PARTS + 1]),
     ]
-    for copy in copies:
+    for copy in copies + block:
         copy.start()
-    pitch = pad.shape[2]
-    rows = pad.reshape(3 * (T + 6) * pitch, g.R)
     for c in range(3):
         for i in range(3):
-            first = c * (T + 6) * pitch
-            rows[pl.ds(first + 5 + i, T + 6, stride=pitch), :] = zlo[c, i]
-            rows[pl.ds(first + 8 + Z + i, T + 6, stride=pitch), :] = zhi[c, i]
+            for z, face, low, high in (
+                (5 + i, zlo, corners[0], corners[2]),
+                (8 + Z + i, zhi, corners[1], corners[3]),
+            ):
+                put_columns(pad, (c,), 0, z, low[c, i])
+                put_columns(pad, (c,), 3, z, face[c, i])
+                put_columns(pad, (c,), T + 3, z, high[c, i])
     for copy in copies:
         copy.wait()
+    return block
 
 
 PAIRS = ((0, 0), (1, 1), (2, 2), (0, 1), (0, 2), (1, 2))
 
 
-def sums_kernel(g, v, tlo, thi, zlo, zhi, width, out, pad, raw, last, pair, acc, sems):
-    fill_pad(g, v, tlo, thi, zlo, zhi, pad, sems)
+def germano_pass(g, fetch, first, count, raws, filters, refs, unit=1, before=None):
+    raw, last, pair, acc = refs
     _, inverse, up, down = g.lanes()
     rows = (inverse, up, down, g.kt * inverse)
-    acc[...] = jnp.zeros_like(acc)
-
-    def step(t, slot):
-        for zc in range(round_up(g.Z + 2, 8) // 8):
-            z = 7 + 8 * zc
-            u, s = strain_rows(pad, t + 2, z, g, rows)
+    index = lax.broadcasted_iota(jnp.int32, (8, g.R), 0)
+
+    def products(t, slot):
+        for z, place in raws:
+            u, s = strain_rows(fetch, t, z, g, rows)
             size = size_of(s)
-            here = pl.ds(8 * zc, 8)
+            here = pl.ds(place, 8)
             for n, (a, b) in enumerate(PAIRS):
                 raw[slot, n, here, :] = u[a] * u[b]
                 raw[slot, 6 + n, here, :] = s[n]
                 raw[slot, 12 + n, here, :] = size * s[n]
-        live = t >= 2
-
-        def smooth(n, load, zc):
-            centre = load(1)
-            h = (load(0) + load(2)) + (centre + centre)
-            here = pl.ds(8 * zc, 8)
-            two = last[n, here, :] + h
-            result = pair[n, here, :] + two
-            last[n, here, :] = h
-            pair[n, here, :] = two
-            return result
-
-        for zc in range(g.Z // 8):
-            mean = [
-                smooth(c, lambda d, c=c: pad[c, t + 2, 7 + 8 * zc + d : 15 + 8 * zc + d, :], zc)
-                for c in range(3)
-            ]
+
+    def smooth(n, load, m):
+        centre = load(1)
+        h = (load(0) + load(2)) + (centre + centre)
+        here = pl.ds(8 * m, 8)
+        two = last[n, here, :] + h
+        result = pair[n, here, :] + two
+        last[n, here, :] = h
+        pair[n, here, :] = two
+        return result
+
+    def contract(i, t, slot):
+        for m, (z, place, keep) in enumerate(filters):
+            mean = [smooth(c, lambda d, c=c: fetch(c, t, z - 1 + d), m) for c in range(3)]
             field = lambda n: smooth(
-                3 + n, lambda d: raw[slot, n, 8 * zc + d : 8 * zc + d + 8, :], zc
+                3 + n, lambda d: raw[slot, n, place + d : place + d + 8, :], m
             )
-            scaled = [m * 0.0625 for m in mean]
+            scaled = [f * 0.0625 for f in mean]
             leonard = [field(n) - scaled[a] * mean[b] for n, (a, b) in enumerate(PAIRS)]
             calm = [field(6 + n) for n in range(6)]
             size = size_of(calm) * (filter_ratio / 16.0)
@@ -183,10 +193,114 @@
                 numer = numer + leonard[n] * model[n]
             diag = model[0] * model[0] + model[1] * model[1] + model[2] * model[2]
             side = model[3] * model[3] + model[4] * model[4] + model[5] * model[5]
+            live = index < jnp.where((i >= 2) & (i < count + 2), keep, 0)
             acc[0] += jnp.where(live, numer, 0.0)
             acc[1] += jnp.where(live, diag + 0.5 * side, 0.0)
 
-    loop(g.T + 2, UNROLL_SUMS, step)
+    def step(i, carry):
+        if before is not None:
+            before(i)
+        for slot in range(unit):
+            products(first - 1 + i * unit + slot, slot)
+        for slot in range(unit):
+            contract(i * unit + slot, first - 1 + i * unit + slot, slot)
+        return carry
+
+    lax.fori_loop(0, (count + 1 + unit) // unit, step, 0)
+
+
+def row_copies(source, target, first, sems):
+    part = source.shape[1] // PARTS
+    return [
+        pltpu.make_async_copy(
+            source.at[:, pl.ds(p * part, part), :, :],
+            target.at[:, pl.ds(first + p * part, part), pl.ds(0 if first == 0 else 8, source.shape[2]), :],
+            sems.at[p],
+        )
+        for p in range(PARTS)
+    ]
+
+
+def inner_kernel(g, source, out, v, raw, last, pair, sems):
+    copies = row_copies(source, v, 0, sems)
+    for copy in copies:
+        copy.start()
+    out[...] = jnp.zeros_like(out)
+    starts = list(range(3, g.Z - 9, 8)) + [g.Z - 9]
+    part = g.T // PARTS
+    copies[0].wait()
+
+    def before(i):
+        for p in range(1, PARTS):
+            pl.when(i == p * part - 2)(copies[p].wait)
+
+    germano_pass(
+        g,
+        lambda c, t, z: v[c, t, z : z + 8, :],
+        2,
+        g.T - 4,
+        [(z, z - 3) for z in starts],
+        [(4 + 8 * m, 8 * m, 8) for m in range(g.Z // 8 - 1)],
+        (raw, last, pair, out),
+        before=before,
+    )
+
+
+def edge_kernel(g, v, *refs):
+    edges, (inner, width, out) = refs[:8], refs[8:11]
+    ends, strip, raw, last, pair, acc, sems = refs[11:]
+    low, high = ends.at[0], ends.at[1]
+    T, Z = g.T, g.Z
+    tlo, thi, zlo, zhi, *corners = edges
+    wide = pl.ds(8, Z)
+    pieces = (
+        (v.at[:, :, pl.ds(0, 8), :], strip.at[:, pl.ds(0, T), pl.ds(8, 8), :]),
+        (v.at[:, :, pl.ds(Z - 8, 8), :], strip.at[:, pl.ds(0, T), pl.ds(16, 8), :]),
+        (tlo, low.at[:, pl.ds(0, 3), wide, :]),
+        (v.at[:, pl.ds(0, 4), :, :], low.at[:, pl.ds(3, 4), wide, :]),
+        (v.at[:, pl.ds(T - 4, 4), :, :], high.at[:, pl.ds(1, 4), wide, :]),
+        (thi, high.at[:, pl.ds(5, 3), wide, :]),
+    )
+    copies = [pltpu.make_async_copy(a, b, sems.at[n]) for n, (a, b) in enumerate(pieces)]
+    for copy in copies:
+        copy.start()
+    for c in range(3):
+        for i in range(3):
+            for n, face in enumerate((zlo, zhi)):
+                put_columns(strip, (c,), 0, (5, 24)[n] + i, face[c, i])
+                z = (5, 8 + Z)[n] + i
+                put_columns(ends, (0, c), 0, z, corners[n][c, i])
+                put_columns(ends, (0, c), 3, z, face[c, i, :4])
+                put_columns(ends, (1, c), 1, z, face[c, i, T - 4 :])
+                put_columns(ends, (1, c), 5, z, corners[2 + n][c, i])
+    acc[...] = inner[...]
+    for copy in copies:
+        copy.wait()
+    work = (raw, last, pair, acc)
+
+    def near(c, t, z):
+        place = z + 8 if z < Z // 2 else z - Z + 24
+        return strip[c, t, place : place + 8, :]
+
+    germano_pass(
+        g,
+        near,
+        2,
+        T - 4,
+        [(-1, 0), (Z - 5, 16)],
+        [(0, 0, 4), (Z - 4, 16, 4)],
+        work,
+        unit=SLOTS,
+    )
+    raws = [(8 * k - 1, 8 * k) for k in range(Z // 8 + 1)]
+    filters = [(8 * m, 8 * m, 8) for m in range(Z // 8)]
+
+    def end(which, carry):
+        fetch = lambda c, t, z: ends[which, c, t + 3, z + 8 : z + 16, :]
+        germano_pass(g, fetch, 0, 2, raws, filters, work)
+        return carry
+
+    lax.fori_loop(0, 2, end, 0)
     w = width[...] * (2.0 / 16.0)
     numer = jnp.sum(acc[0], axis=0, keepdims=True) * (w[:1] * (1.0 / 16.0))
     denom = jnp.sum(acc[1], axis=0, keepdims=True) * (w[:1] * w[:1])
@@ -194,11 +308,13 @@
     out[...] = jnp.where(index == 0, numer, jnp.where(index == 1, denom, 0.0))
 
 
-def source_kernel(g, v, tlo, thi, zlo, zhi, width, sums, ratio, *rest):
+def source_kernel(g, v, *refs):
+    edges, (width, sums, ratio), rest = refs[:8], refs[8:11], refs[11:]
     outs = rest[: g.chunks * g.ng]
     pad, tau, eddy, vt, vz, src, flip, sems, osems = rest[g.chunks * g.ng :]
     T, Z, R = g.T, g.Z, g.R
-    fill_pad(g, v, tlo, thi, zlo, zhi, pad, sems)
+    block = fill_pad(g, v, edges, pad, sems)
+    block[0].wait()
     radius, inverse, up, down = g.lanes()
     rows = (inverse, up, down, g.kt * inverse)
     kt = rows[3]
@@ -206,10 +322,11 @@
     coefficient = total[0:1] / (total[1:2] + epsilon_den)
     strength = jnp.broadcast_to(coefficient, (8, R)) * width[...]
 
+    fetch = lambda c, t, z: pad[c, t + 3, z + 8 : z + 16, :]
+
     def stress_row(t, slot):
         for zc in range(eddy.shape[1] // 8):
-            z = 6 + 8 * zc
-            _, s = strain_rows(pad, t + 1, z, g, rows)
+            _, s = strain_rows(fetch, t - 2, 8 * zc - 2, g, rows)
             e = strength * size_of(s)
             here = pl.ds(8 * zc, 8)
             eddy[t, here, :] = e * (1.0 / nu_molecular)
@@ -219,7 +336,11 @@
                 tau[n, t, here, :] = main * s[n]
                 tau[3 + n, t, here, :] = side * s[3 + n]
 
-    loop(T + 4, UNROLL, stress_row)
+    def arrived(i, unit):
+        for p in range(1, PARTS):
+            pl.when(i == -(-(p * (T // PARTS) + 2 - unit) // unit))(block[p].wait)
+
+    loop(T + 4, UNROLL, stress_row, arrived)
 
     def slab(n, t, z):
         return tau[n, t, z : z + 8, :]
@@ -475,17 +596,26 @@
 def halo(g, v):
     T, Z = g.T, g.Z
 
-    def pair(low, high, axis, count):
-        forward = [(i, (i + 1) % count) for i in range(count)]
-        backward = [(target, source) for source, target in forward]
-        return lax.ppermute(high, axis, forward), lax.ppermute(low, axis, backward)
-
-    tlo, thi = pair(v[:, :3], v[:, T - 3 :], "theta", g.nt)
-    face = lambda first: jnp.concatenate(
-        [f[:, :, first : first + 3].transpose(0, 2, 1, 3) for f in (tlo, v, thi)], axis=2
-    )
-    zlo, zhi = pair(face(0), face(Z - 3), "gz", g.ng)
-    return tlo, thi, zlo, zhi
+    def move(block, dt, dz):
+        ring = [
+            (t * g.ng + z, (t + dt) % g.nt * g.ng + (z + dz) % g.ng)
+            for t in range(g.nt)
+            for z in range(g.ng)
+        ]
+        return lax.ppermute(block, ("theta", "gz"), ring)
+
+    first = v[:, :, :3].transpose(0, 2, 1, 3)
+    final = v[:, :, Z - 3 :].transpose(0, 2, 1, 3)
+    faces = [
+        move(final, 0, 1), move(first, 0, -1), move(v[:, T - 3 :], 1, 0), move(v[:, :3], -1, 0)
+    ]
+    corners = [
+        move(final[:, :, T - 3 :], 1, 1),
+        move(first[:, :, T - 3 :], 1, -1),
+        move(final[:, :, :3], -1, 1),
+        move(first[:, :, :3], -1, -1),
+    ]
+    return faces[2], faces[3], faces[0], faces[1], *corners
 
 
 def axial_table(g):
@@ -538,23 +668,32 @@
     edges = halo(g, velocity)
     width = width_row(g)
     pad = buf(3, T + 6, odd_tiles(Z + 16), R)
-    halo_specs = [ANY, ANY, ANY, VM, VM, VM]
+    halo_specs = [ANY, ANY, ANY] + [VM] * 6
+    work = [buf(SLOTS, 18, odd_tiles(Z + 2), R), buf(21, odd_tiles(Z), R), buf(21, odd_tiles(Z), R)]
+    inner = pl.pallas_call(
+        functools.partial(inner_kernel, g),
+        out_shape=shape(2, 8, R),
+        in_specs=[ANY],
+        out_specs=VM,
+        scratch_shapes=[buf(3, T, Z, R), *work, dma((PARTS,))],
+        compiler_params=params(50 * 1024 * 1024),
+        name="inner_sums",
+    )(velocity)
     part = pl.pallas_call(
-        functools.partial(sums_kernel, g),
+        functools.partial(edge_kernel, g),
         out_shape=shape(8, R),
-        in_specs=halo_specs,
+        in_specs=[ANY, ANY, ANY] + [VM] * 8,
         out_specs=VM,
         scratch_shapes=[
-            pad,
-            buf(UNROLL_SUMS, 18, odd_tiles(Z + 2), R),
-            buf(21, odd_tiles(Z), R),
-            buf(21, odd_tiles(Z), R),
+            buf(2, 3, 8, odd_tiles(Z + 16), R),
+            buf(3, T + 2, 40, R),
+            *work,
             buf(2, 8, R),
-            dma((3,)),
+            dma((6,)),
         ],
-        compiler_params=params(),
-        name="germano_sums",
-    )(velocity, *edges, width)
+        compiler_params=params(40 * 1024 * 1024),
+        name="edge_sums",
+    )(velocity, *edges, inner, width)
     count = g.nt * g.ng
     sums = lax.all_to_all(
         jnp.broadcast_to(part[None], (count, 8, R)), ("theta", "gz"), 0, 0, tiled=True
@@ -563,7 +702,7 @@
         functools.partial(source_kernel, g),
         out_shape=[shape(T, Z, R)]
         + [shape(rb, Z // 2, 2 * T) for rb in g.rb for _ in range(g.ng)],
-        in_specs=halo_specs + [VM],
+        in_specs=halo_specs + [VM] * 2,
         out_specs=[VM] + [ANY] * (g.chunks * g.ng),
         scratch_shapes=[
             pad,
@@ -573,7 +712,7 @@
             buf(T, round_up(Z + 2, 8), R),
             buf(T, Z + 8, R),
             buf(R, Z // 2 + 8, 2 * T),
-            dma((3,)),
+            dma((PARTS + 2,)),
             dma((g.chunks * g.ng,)),
         ],
         compiler_params=params(),

time: 269 us -> 258 us (0.959)
  the two profiles are of different devices: /device:TPU:0 before, /device:TPU:15 now
where the time goes in v2:
time: 258 us; the launch traced here: 256 us
  Pallas kernels  84.2 us (33%)
  waiting for transfers between devices  79.2 us (31%)
  starting transfers between devices  69.5 us (27%)
  blocking collectives  13.9 us (5%)
  local copies, waits for them, and re-layouts  5.54 us (2%)
    ppermute x52, starting transfers between devices, exchange(): received.append(lax.ppermute(blocks[s], axis, ring))  62.1 us
    ppermute x52, waiting for transfers between devices, exchange(): received.append(lax.ppermute(blocks[s], axis, ring))  61.1 us
    pallas_call x1, Pallas kernels, program(): pl.pallas_call(functools.partial(source_kernel, g), out_shape=[shape(T, Z...  22.7 us
    pallas_call x1, Pallas kernels, program(): pl.pallas_call(functools.partial(inner_kernel, g), out_shape=shape(2, 8,...  21.3 us
    ppermute x8, waiting for transfers between devices, move(): return lax.ppermute(block, ('theta', 'gz'), ring)  18.1 us
    all_to_all x1, blocking collectives, program(): lax.all_to_all(jnp.broadcast_to(part[None], (count, 8, R)), ('theta', 'gz...  13.9 us
    pallas_call x4, Pallas kernels, program(): pl.pallas_call(functools.partial(turn_kernel, g, rb), out_shape=[shape(2,...  13.7 us
    pallas_call x4, Pallas kernels, program(): pl.pallas_call(functools.partial(axial_kernel, g, rb), out_shape=[shape(r...  10.9 us
  transfers between devices with their start and end apart: 60, of which 27 were waited for; matrix products, arithmetic and copies ran while one was open for 1% of the time, Pallas kernels for 17%

profile of v2, /device:TPU:15, one launch (start us, length us, event | category | flops | bytes accessed | tf_op | source)
XLA Modules:
  0.0 255.5 jit_solution(4990822025285775027)
XLA Ops:
  6.9 3.2 %collective-permute-start.4 = (f32[3,3,3,128]{3,2,1,0:T(4,128)S(1)}, f32[3,3,3,128]{3,2,1,0:T(4,128)S(1)}, u32[]{:S(2)}, u32[]{:S(2)}) collective-permute-start(f32[3,3,3,128]{3,2,1,0:T(4,128)S(1)} %get-tuple-element.217), channel_id=1, source_target_pairs={{0,5},{1,6},{2,7},{3,4},{4,9},{5,10},{6,11},{7,8},{8,13},{9,14},{1... | collective-permute-start | bytes 41480 | tf_op jit(solution)/shard_map/ppermute | solution.py:605
  10.0 10.8 %collective-permute-done.4.refs_4_ = f32[3,3,3,128]{3,2,1,0:T(4,128)S(1)} collective-permute-done((f32[3,3,3,128]{3,2,1,0:T(4,128)S(1)}, f32[3,3,3,128]{3,2,1,0:T(4,128)S(1)}, u32[]{:S(2)}, u32[]{:S(2)}) %collective-permute-start.4) | collective-permute-done | bytes 13856 | tf_op jit(solution)/shard_map/ppermute | solution.py:605
  21.6 3.3 %collective-permute-done.5.refs_5_ = f32[3,3,3,128]{3,2,1,0:T(4,128)S(1)} collective-permute-done((f32[3,3,3,128]{3,2,1,0:T(4,128)S(1)}, f32[3,3,3,128]{3,2,1,0:T(4,128)S(1)}, u32[]{:S(2)}, u32[]{:S(2)}) %collective-permute-start.5) | collective-permute-done | bytes 13856 | tf_op jit(solution)/shard_map/ppermute | solution.py:605
  24.9 4.1 %collective-permute-done.6.refs_6_ = f32[3,3,3,128]{3,2,1,0:T(4,128)S(1)} collective-permute-done((f32[3,3,3,128]{3,2,1,0:T(4,128)S(1)}, f32[3,3,3,128]{3,2,1,0:T(4,128)S(1)}, u32[]{:S(2)}, u32[]{:S(2)}) %collective-permute-start.6) | collective-permute-done | bytes 13856 | tf_op jit(solution)/shard_map/ppermute | solution.py:605
  29.0 21.3 %inner_sums.1.refs_8_ = f32[2,8,128]{2,1,0:T(8,128)S(1)} custom-call(f32[3,64,64,128]{3,2,1,0:T(8,128)} %v.3), custom_call_target="tpu_custom_call" | custom-call | tf_op jit(solution)/shard_map/inner_sums/pallas_call | solution.py:673
  50.5 9.0 %edge_sums.1 = f32[8,128]{1,0:T(8,128)S(1)} custom-call(f32[3,64,64,128]{3,2,1,0:T(8,128)S(1)} %copy-done, f32[3,3,64,128]{3,2,1,0:T(8,128)S(1)} %collective-permute-done.refs_0_, f32[3,3,64,128]{3,2,1,0:T(8,128)S(1)} %collective-permute-done.1.refs_1_, f32[3,3,64,128]{3,2,1,0:T(8,128)S(1)} %collective-permute-done.2.refs_2_, ...), custom_call_target="tpu_custom_call" | custom-call | tf_op jit(solution)/shard_map/edge_sums/pallas_call | solution.py:682
  59.6 13.9 %all_to_all.5.refs_9_ = f32[32,8,128]{2,1,0:T(8,128)} all-to-all(f32[32,8,128]{2,1,0:T(8,128)S(1)} %broadcast_in_dim.2), channel_id=1, replica_groups=mesh['theta'=8,'gz'=4] {'theta','gz'}, dimensions={0} | all-to-all | bytes 262144 | tf_op jit(solution)/shard_map/all_to_all | solution.py:698
  73.5 22.7 %source.3 = (f32[64,64,128]{2,1,0:T(8,128)}, f32[8,32,128]{2,1,0:T(8,128)}, f32[8,32,128]{2,1,0:T(8,128)}, f32[8,32,128]{2,1,0:T(8,128)}, f32[8,32,128]{2,1,0:T(...) custom-call(f32[3,64,64,128]{3,2,1,0:T(8,128)} %v.3, ...), custom_call_target="tpu_custom_call" | custom-call | tf_op jit(solution)/shard_map/source/pallas_call | solution.py:701
  114.4 3.2 %collective-permute-start.13 = (f32[8,32,128]{2,1,0:T(8,128)S(1)}, f32[8,32,128]{2,1,0:T(8,128)S(1)}, u32[]{:S(2)}, u32[]{:S(2)}) collective-permute-start(f32[8,32,128]{2,1,0:T(8,128)S(1)} %get-tuple-element.123), channel_id=1, source_target_pairs={{0,12},{4,16},{8,20},{12,24},{16,28},{20,0},{24,4},{28,8},{1,13},{... | collective-permute-start | bytes 393224 | tf_op jit(solution)/shard_map/ppermute | solution.py:587
  131.1 4.3 %collective-permute-start.16 = (f32[8,32,128]{2,1,0:T(8,128)S(1)}, f32[8,32,128]{2,1,0:T(8,128)S(1)}, u32[]{:S(2)}, u32[]{:S(2)}) collective-permute-start(f32[8,32,128]{2,1,0:T(8,128)S(1)} %get-tuple-element.126), channel_id=1, source_target_pairs={{0,24},{4,28},{8,0},{12,4},{16,8},{20,12},{24,16},{28,20},{1,25},{... | collective-permute-start | bytes 393224 | tf_op jit(solution)/shard_map/ppermute | solution.py:587
  147.3 12.0 %collective-permute-done.26.refs_3_ = f32[8,32,128]{2,1,0:T(8,128)S(1)} collective-permute-done((f32[8,32,128]{2,1,0:T(8,128)S(1)}, f32[8,32,128]{2,1,0:T(8,128)S(1)}, u32[]{:S(2)}, u32[]{:S(2)}) %collective-permute-start.26) | collective-permute-done | bytes 131104 | tf_op jit(solution)/shard_map/ppermute | solution.py:587
  169.0 3.4 %turn_modes.4 = (f32[2,8,32,128]{3,2,1,0:T(8,128)S(1)}, f32[2,8,32,128]{3,2,1,0:T(8,128)S(1)}, f32[2,8,32,128]{3,2,1,0:T(8,128)S(1)}, f32[2,8,32,128]{3,2,1,0:T(8,128)S(1)}) custom-call(f32[8,32,128]{2,1,0:T(8,128)S(1)} %get-tuple-element.120.refs_0_, f32[8,32,128]{2,1,0:T(8,128)S(1)} %collective-permute-done.11.refs_1_, ...), custom_call_target="tpu_custom_call" | custom-call | tf_op jit(solution)/shard_map/turn_modes/pallas_call | solution.py:742
  177.4 3.2 %collective-permute-start.41 = (f32[8,32,128]{2,1,0:T(8,128)S(1)}, f32[8,32,128]{2,1,0:T(8,128)S(1)}, u32[]{:S(2)}, u32[]{:S(2)}) collective-permute-start(f32[8,32,128]{2,1,0:T(8,128)S(1)} %get-tuple-element.181), channel_id=1, source_target_pairs={{0,20},{4,24},{8,28},{12,0},{16,4},{20,8},{24,12},{28,16},{1,21},{... | collective-permute-start | bytes 393224 | tf_op jit(solution)/shard_map/ppermute | solution.py:587
  189.1 4.9 %collective-permute-start.52 = (f32[8,32,128]{2,1,0:T(8,128)S(1)}, f32[8,32,128]{2,1,0:T(8,128)S(1)}, u32[]{:S(2)}, u32[]{:S(2)}) collective-permute-start(f32[8,32,128]{2,1,0:T(8,128)S(1)} %get-tuple-element.195), channel_id=1, source_target_pairs={{0,12},{4,16},{8,20},{12,24},{16,28},{20,0},{24,4},{28,8},{1,13},{... | collective-permute-start | bytes 393224 | tf_op jit(solution)/shard_map/ppermute | solution.py:587
  198.9 3.4 %turn_modes.5 = (f32[2,8,32,128]{3,2,1,0:T(8,128)S(1)}, f32[2,8,32,128]{3,2,1,0:T(8,128)S(1)}, f32[2,8,32,128]{3,2,1,0:T(8,128)S(1)}, f32[2,8,32,128]{3,2,1,0:T(8,128)S(1)}) custom-call(f32[8,32,128]{2,1,0:T(8,128)S(1)} %get-tuple-element.148.refs_0_, f32[8,32,128]{2,1,0:T(8,128)S(1)} %collective-permute-done.24.refs_1_, ...), custom_call_target="tpu_custom_call" | custom-call | tf_op jit(solution)/shard_map/turn_modes/pallas_call | solution.py:742
  202.4 3.4 %turn_modes.6 = (f32[2,8,32,128]{3,2,1,0:T(8,128)S(1)}, f32[2,8,32,128]{3,2,1,0:T(8,128)S(1)}, f32[2,8,32,128]{3,2,1,0:T(8,128)S(1)}, f32[2,8,32,128]{3,2,1,0:T(8,128)S(1)}) custom-call(f32[8,32,128]{2,1,0:T(8,128)S(1)} %get-tuple-element.176.refs_0_, f32[8,32,128]{2,1,0:T(8,128)S(1)} %collective-permute-done.37.refs_1_, ...), custom_call_target="tpu_custom_call" | custom-call | tf_op jit(solution)/shard_map/turn_modes/pallas_call | solution.py:742
  205.9 5.1 %collective-permute-done.53.refs_4_ = f32[8,32,128]{2,1,0:T(8,128)S(1)} collective-permute-done((f32[8,32,128]{2,1,0:T(8,128)S(1)}, f32[8,32,128]{2,1,0:T(8,128)S(1)}, u32[]{:S(2)}, u32[]{:S(2)}) %collective-permute-start.53) | collective-permute-done | bytes 131104 | tf_op jit(solution)/shard_map/ppermute | solution.py:587
  212.3 5.0 %collective-permute-done.55.refs_6_ = f32[8,32,128]{2,1,0:T(8,128)S(1)} collective-permute-done((f32[8,32,128]{2,1,0:T(8,128)S(1)}, f32[8,32,128]{2,1,0:T(8,128)S(1)}, u32[]{:S(2)}, u32[]{:S(2)}) %collective-permute-start.55) | collective-permute-done | bytes 131104 | tf_op jit(solution)/shard_map/ppermute | solution.py:587
  219.6 3.4 %turn_modes.7 = (f32[2,8,32,128]{3,2,1,0:T(8,128)S(1)}, f32[2,8,32,128]{3,2,1,0:T(8,128)S(1)}, f32[2,8,32,128]{3,2,1,0:T(8,128)S(1)}, f32[2,8,32,128]{3,2,1,0:T(8,128)S(1)}) custom-call(f32[8,32,128]{2,1,0:T(8,128)S(1)} %get-tuple-element.192.refs_0_, f32[8,32,128]{2,1,0:T(8,128)S(1)} %collective-permute-done.50.refs_1_, ...), custom_call_target="tpu_custom_call" | custom-call | tf_op jit(solution)/shard_map/turn_modes/pallas_call | solution.py:742
  227.0 4.5 %collective-permute-done.44.refs_9_ = f32[2,8,32,128]{3,2,1,0:T(8,128)S(1)} collective-permute-done((f32[2,8,32,128]{3,2,1,0:T(8,128)S(1)}, f32[2,8,32,128]{3,2,1,0:T(8,128)S(1)}, u32[]{:S(2)}, u32[]{:S(2)}) %collective-permute-start.44) | collective-permute-done | bytes 262176 | tf_op jit(solution)/shard_map/ppermute | solution.py:587
  232.2 5.3 %collective-permute-done.46.refs_11_ = f32[2,8,32,128]{3,2,1,0:T(8,128)S(1)} collective-permute-done((f32[2,8,32,128]{3,2,1,0:T(8,128)S(1)}, f32[2,8,32,128]{3,2,1,0:T(8,128)S(1)}, u32[]{:S(2)}, u32[]{:S(2)}) %collective-permute-start.46) | collective-permute-done | bytes 262176 | tf_op jit(solution)/shard_map/ppermute | solution.py:587
  237.5 5.3 %collective-permute-done.57.refs_13_ = f32[2,8,32,128]{3,2,1,0:T(8,128)S(1)} collective-permute-done((f32[2,8,32,128]{3,2,1,0:T(8,128)S(1)}, f32[2,8,32,128]{3,2,1,0:T(8,128)S(1)}, u32[]{:S(2)}, u32[]{:S(2)}) %collective-permute-start.57) | collective-permute-done | bytes 262176 | tf_op jit(solution)/shard_map/ppermute | solution.py:587
  243.5 5.3 %collective-permute-done.59.refs_15_ = f32[2,8,32,128]{3,2,1,0:T(8,128)S(1)} collective-permute-done((f32[2,8,32,128]{3,2,1,0:T(8,128)S(1)}, f32[2,8,32,128]{3,2,1,0:T(8,128)S(1)}, u32[]{:S(2)}, u32[]{:S(2)}) %collective-permute-start.59) | collective-permute-done | bytes 262176 | tf_op jit(solution)/shard_map/ppermute | solution.py:587
  248.8 6.6 %solve_modes.1 = f32[2,128,32,128]{3,2,1,0:T(8,128)} custom-call(f32[2,8,32,128]{3,2,1,0:T(8,128)S(1)} %get-tuple-element.128.refs_0_, f32[2,8,32,128]{3,2,1,0:T(8,128)S(1)} %collective-permute-done.18.refs_1_, f32[2,8,32,128]{3,2,1,0:T(8,128)S(1)} %collective-permute-done.19.refs_2_, f32[2,8,32,128]{3,2,1,0:T(8,128)S(1)} %collective-permute-done.20.refs_3_, ...), custom_call_target="tpu_custom_call" | custom-call | tf_op jit(solution)/shard_map/solve_modes/pallas_call | solution.py:751
  (171 shorter events, 87.6 us)
Async XLA Ops:
  1.7 48.6 %collective-permute-start = (f32[3,3,64,128]{3,2,1,0:T(8,128)S(1)}, f32[3,3,64,128]{3,2,1,0:T(8,128)S(1)}, u32[]{:S(2)}, u32[]{:S(2)}) collective-permute-start(f32[3,3,64,128]{3,2,1,0:T(8,128)S(1)} %get-tuple-element.207), channel_id=1, source_target_pairs={{0,4},{1,5},{2,6},{3,7},{4,8},{5,9},{6,10},{7,11},{8,12},{9,13},{1... | collective-permute-start | bytes 884744 | tf_op jit(solution)/shard_map/ppermute | solution.py:605
  3.6 46.7 %collective-permute-start.1 = (f32[3,3,64,128]{3,2,1,0:T(8,128)S(1)}, f32[3,3,64,128]{3,2,1,0:T(8,128)S(1)}, u32[]{:S(2)}, u32[]{:S(2)}) collective-permute-start(f32[3,3,64,128]{3,2,1,0:T(8,128)S(1)} %get-tuple-element.206), channel_id=1, source_target_pairs={{0,28},{1,29},{2,30},{3,31},{4,0},{5,1},{6,2},{7,3},{8,4},{9,5},{1... | collective-permute-start | bytes 884744 | tf_op jit(solution)/shard_map/ppermute | solution.py:605
  5.2 45.1 %collective-permute-start.2 = (f32[3,3,64,128]{3,2,1,0:T(8,128)S(1)}, f32[3,3,64,128]{3,2,1,0:T(8,128)S(1)}, u32[]{:S(2)}, u32[]{:S(2)}) collective-permute-start(f32[3,3,64,128]{3,2,1,0:T(8,128)S(1)} %bitcast.6), channel_id=1, source_target_pairs={{0,1},{1,2},{2,3},{3,0},{4,5},{5,6},{6,7},{7,4},{8,9},{9,10},{10,1... | collective-permute-start | bytes 884744 | tf_op jit(solution)/shard_map/ppermute | solution.py:605
  5.5 44.9 %collective-permute-start.3 = (f32[3,3,64,128]{3,2,1,0:T(8,128)S(1)}, f32[3,3,64,128]{3,2,1,0:T(8,128)S(1)}, u32[]{:S(2)}, u32[]{:S(2)}) collective-permute-start(f32[3,3,64,128]{3,2,1,0:T(8,128)S(1)} %bitcast.8), channel_id=1, source_target_pairs={{0,3},{1,0},{2,1},{3,2},{4,7},{5,4},{6,5},{7,6},{8,11},{9,8},{10,9... | collective-permute-start | bytes 884744 | tf_op jit(solution)/shard_map/ppermute | solution.py:605
  6.9 13.9 %collective-permute-start.4 = (f32[3,3,3,128]{3,2,1,0:T(4,128)S(1)}, f32[3,3,3,128]{3,2,1,0:T(4,128)S(1)}, u32[]{:S(2)}, u32[]{:S(2)}) collective-permute-start(f32[3,3,3,128]{3,2,1,0:T(4,128)S(1)} %get-tuple-element.217), channel_id=1, source_target_pairs={{0,5},{1,6},{2,7},{3,4},{4,9},{5,10},{6,11},{7,8},{8,13},{9,14},{1... | collective-permute-start | bytes 41480 | tf_op jit(solution)/shard_map/ppermute | solution.py:605
  29.0 21.4 %collective-permute-start.7 = (f32[3,3,3,128]{3,2,1,0:T(4,128)S(1)}, f32[3,3,3,128]{3,2,1,0:T(4,128)S(1)}, u32[]{:S(2)}, u32[]{:S(2)}) collective-permute-start(f32[3,3,3,128]{3,2,1,0:T(4,128)S(1)} %get-tuple-element.214), channel_id=1, source_target_pairs={{0,31},{1,28},{2,29},{3,30},{4,3},{5,0},{6,1},{7,2},{8,7},{9,4},{1... | collective-permute-start | bytes 41480 | tf_op jit(solution)/shard_map/ppermute | solution.py:605
  119.0 16.4 %collective-permute-start.15 = (f32[8,32,128]{2,1,0:T(8,128)S(1)}, f32[8,32,128]{2,1,0:T(8,128)S(1)}, u32[]{:S(2)}, u32[]{:S(2)}) collective-permute-start(f32[8,32,128]{2,1,0:T(8,128)S(1)} %get-tuple-element.125), channel_id=1, source_target_pairs={{0,20},{4,24},{8,28},{12,0},{16,4},{20,8},{24,12},{28,16},{1,21},{... | collective-permute-start | bytes 393224 | tf_op jit(solution)/shard_map/ppermute | solution.py:587
  138.3 21.1 %collective-permute-start.26 = (f32[8,32,128]{2,1,0:T(8,128)S(1)}, f32[8,32,128]{2,1,0:T(8,128)S(1)}, u32[]{:S(2)}, u32[]{:S(2)}) collective-permute-start(f32[8,32,128]{2,1,0:T(8,128)S(1)} %get-tuple-element.151), channel_id=1, source_target_pairs={{0,12},{4,16},{8,20},{12,24},{16,28},{20,0},{24,4},{28,8},{1,13},{... | collective-permute-start | bytes 393224 | tf_op jit(solution)/shard_map/ppermute | solution.py:587
  142.6 19.6 %collective-permute-start.27 = (f32[8,32,128]{2,1,0:T(8,128)S(1)}, f32[8,32,128]{2,1,0:T(8,128)S(1)}, u32[]{:S(2)}, u32[]{:S(2)}) collective-permute-start(f32[8,32,128]{2,1,0:T(8,128)S(1)} %get-tuple-element.152), channel_id=1, source_target_pairs={{0,16},{4,20},{8,24},{12,28},{16,0},{20,4},{24,8},{28,12},{1,17},{... | collective-permute-start | bytes 393224 | tf_op jit(solution)/shard_map/ppermute | solution.py:587
  144.9 18.7 %collective-permute-start.28 = (f32[8,32,128]{2,1,0:T(8,128)S(1)}, f32[8,32,128]{2,1,0:T(8,128)S(1)}, u32[]{:S(2)}, u32[]{:S(2)}) collective-permute-start(f32[8,32,128]{2,1,0:T(8,128)S(1)} %get-tuple-element.153), channel_id=1, source_target_pairs={{0,20},{4,24},{8,28},{12,0},{16,4},{20,8},{24,12},{28,16},{1,21},{... | collective-permute-start | bytes 393224 | tf_op jit(solution)/shard_map/ppermute | solution.py:587
  146.9 17.9 %collective-permute-start.29 = (f32[8,32,128]{2,1,0:T(8,128)S(1)}, f32[8,32,128]{2,1,0:T(8,128)S(1)}, u32[]{:S(2)}, u32[]{:S(2)}) collective-permute-start(f32[8,32,128]{2,1,0:T(8,128)S(1)} %get-tuple-element.154), channel_id=1, source_target_pairs={{0,24},{4,28},{8,0},{12,4},{16,8},{20,12},{24,16},{28,20},{1,25},{... | collective-permute-start | bytes 393224 | tf_op jit(solution)/shard_map/ppermute | solution.py:587
  146.9 18.3 %collective-permute-start.30 = (f32[8,32,128]{2,1,0:T(8,128)S(1)}, f32[8,32,128]{2,1,0:T(8,128)S(1)}, u32[]{:S(2)}, u32[]{:S(2)}) collective-permute-start(f32[8,32,128]{2,1,0:T(8,128)S(1)} %get-tuple-element.155), channel_id=1, source_target_pairs={{0,28},{4,0},{8,4},{12,8},{16,12},{20,16},{24,20},{28,24},{1,29},{... | collective-permute-start | bytes 393224 | tf_op jit(solution)/shard_map/ppermute | solution.py:587
  174.4 19.7 %collective-permute-start.18 = (f32[2,8,32,128]{3,2,1,0:T(8,128)S(1)}, f32[2,8,32,128]{3,2,1,0:T(8,128)S(1)}, u32[]{:S(2)}, u32[]{:S(2)}) collective-permute-start(f32[2,8,32,128]{3,2,1,0:T(8,128)S(1)} %get-tuple-element.129), channel_id=1, source_target_pairs={{0,1},{1,2},{2,3},{3,0},{4,5},{5,6},{6,7},{7,4},{8,9},{9,10},{10,1... | collective-permute-start | bytes 786440 | tf_op jit(solution)/shard_map/ppermute | solution.py:587
  176.3 18.4 %collective-permute-start.19 = (f32[2,8,32,128]{3,2,1,0:T(8,128)S(1)}, f32[2,8,32,128]{3,2,1,0:T(8,128)S(1)}, u32[]{:S(2)}, u32[]{:S(2)}) collective-permute-start(f32[2,8,32,128]{3,2,1,0:T(8,128)S(1)} %get-tuple-element.130), channel_id=1, source_target_pairs={{0,2},{1,3},{2,0},{3,1},{4,6},{5,7},{6,4},{7,5},{8,10},{9,11},{10,... | collective-permute-start | bytes 786440 | tf_op jit(solution)/shard_map/ppermute | solution.py:587
  189.1 16.7 %collective-permute-start.52 = (f32[8,32,128]{2,1,0:T(8,128)S(1)}, f32[8,32,128]{2,1,0:T(8,128)S(1)}, u32[]{:S(2)}, u32[]{:S(2)}) collective-permute-start(f32[8,32,128]{2,1,0:T(8,128)S(1)} %get-tuple-element.195), channel_id=1, source_target_pairs={{0,12},{4,16},{8,20},{12,24},{16,28},{20,0},{24,4},{28,8},{1,13},{... | collective-permute-start | bytes 393224 | tf_op jit(solution)/shard_map/ppermute | solution.py:587
  194.1 16.9 %collective-permute-start.53 = (f32[8,32,128]{2,1,0:T(8,128)S(1)}, f32[8,32,128]{2,1,0:T(8,128)S(1)}, u32[]{:S(2)}, u32[]{:S(2)}) collective-permute-start(f32[8,32,128]{2,1,0:T(8,128)S(1)} %get-tuple-element.196), channel_id=1, source_target_pairs={{0,16},{4,20},{8,24},{12,28},{16,0},{20,4},{24,8},{28,12},{1,17},{... | collective-permute-start | bytes 393224 | tf_op jit(solution)/shard_map/ppermute | solution.py:587
  194.7 16.3 %collective-permute-start.54 = (f32[8,32,128]{2,1,0:T(8,128)S(1)}, f32[8,32,128]{2,1,0:T(8,128)S(1)}, u32[]{:S(2)}, u32[]{:S(2)}) collective-permute-start(f32[8,32,128]{2,1,0:T(8,128)S(1)} %get-tuple-element.197), channel_id=1, source_target_pairs={{0,20},{4,24},{8,28},{12,0},{16,4},{20,8},{24,12},{28,16},{1,21},{... | collective-permute-start | bytes 393224 | tf_op jit(solution)/shard_map/ppermute | solution.py:587
  196.7 20.6 %collective-permute-start.55 = (f32[8,32,128]{2,1,0:T(8,128)S(1)}, f32[8,32,128]{2,1,0:T(8,128)S(1)}, u32[]{:S(2)}, u32[]{:S(2)}) collective-permute-start(f32[8,32,128]{2,1,0:T(8,128)S(1)} %get-tuple-element.198), channel_id=1, source_target_pairs={{0,24},{4,28},{8,0},{12,4},{16,8},{20,12},{24,16},{28,20},{1,25},{... | collective-permute-start | bytes 393224 | tf_op jit(solution)/shard_map/ppermute | solution.py:587
  198.5 18.8 %collective-permute-start.56 = (f32[8,32,128]{2,1,0:T(8,128)S(1)}, f32[8,32,128]{2,1,0:T(8,128)S(1)}, u32[]{:S(2)}, u32[]{:S(2)}) collective-permute-start(f32[8,32,128]{2,1,0:T(8,128)S(1)} %get-tuple-element.199), channel_id=1, source_target_pairs={{0,28},{4,0},{8,4},{12,8},{16,12},{20,16},{24,20},{28,24},{1,29},{... | collective-permute-start | bytes 393224 | tf_op jit(solution)/shard_map/ppermute | solution.py:587
  205.8 17.2 %collective-permute-start.20 = (f32[2,8,32,128]{3,2,1,0:T(8,128)S(1)}, f32[2,8,32,128]{3,2,1,0:T(8,128)S(1)}, u32[]{:S(2)}, u32[]{:S(2)}) collective-permute-start(f32[2,8,32,128]{3,2,1,0:T(8,128)S(1)} %get-tuple-element.131), channel_id=1, source_target_pairs={{0,3},{1,0},{2,1},{3,2},{4,7},{5,4},{6,5},{7,6},{8,11},{9,8},{10,9... | collective-permute-start | bytes 786440 | tf_op jit(solution)/shard_map/ppermute | solution.py:587
  217.4 14.1 %collective-permute-start.44 = (f32[2,8,32,128]{3,2,1,0:T(8,128)S(1)}, f32[2,8,32,128]{3,2,1,0:T(8,128)S(1)}, u32[]{:S(2)}, u32[]{:S(2)}) collective-permute-start(f32[2,8,32,128]{3,2,1,0:T(8,128)S(1)} %get-tuple-element.185), channel_id=1, source_target_pairs={{0,1},{1,2},{2,3},{3,0},{4,5},{5,6},{6,7},{7,4},{8,9},{9,10},{10,1... | collective-permute-start | bytes 786440 | tf_op jit(solution)/shard_map/ppermute | solution.py:587
  223.7 19.1 %collective-permute-start.57 = (f32[2,8,32,128]{3,2,1,0:T(8,128)S(1)}, f32[2,8,32,128]{3,2,1,0:T(8,128)S(1)}, u32[]{:S(2)}, u32[]{:S(2)}) collective-permute-start(f32[2,8,32,128]{3,2,1,0:T(8,128)S(1)} %get-tuple-element.201), channel_id=1, source_target_pairs={{0,1},{1,2},{2,3},{3,0},{4,5},{5,6},{6,7},{7,4},{8,9},{9,10},{10,1... | collective-permute-start | bytes 786440 | tf_op jit(solution)/shard_map/ppermute | solution.py:587
  226.2 17.2 %collective-permute-start.58 = (f32[2,8,32,128]{3,2,1,0:T(8,128)S(1)}, f32[2,8,32,128]{3,2,1,0:T(8,128)S(1)}, u32[]{:S(2)}, u32[]{:S(2)}) collective-permute-start(f32[2,8,32,128]{3,2,1,0:T(8,128)S(1)} %get-tuple-element.202), channel_id=1, source_target_pairs={{0,2},{1,3},{2,0},{3,1},{4,6},{5,7},{6,4},{7,5},{8,10},{9,11},{10,... | collective-permute-start | bytes 786440 | tf_op jit(solution)/shard_map/ppermute | solution.py:587
  231.5 17.2 %collective-permute-start.59 = (f32[2,8,32,128]{3,2,1,0:T(8,128)S(1)}, f32[2,8,32,128]{3,2,1,0:T(8,128)S(1)}, u32[]{:S(2)}, u32[]{:S(2)}) collective-permute-start(f32[2,8,32,128]{3,2,1,0:T(8,128)S(1)} %get-tuple-element.203), channel_id=1, source_target_pairs={{0,3},{1,0},{2,1},{3,2},{4,7},{5,4},{6,5},{7,6},{8,11},{9,8},{10,9... | collective-permute-start | bytes 786440 | tf_op jit(solution)/shard_map/ppermute | solution.py:587
  (62 other events, 1344.4 us)

commit v3 on v2

--- a/solution.py
+++ b/solution.py
@@ -14,7 +14,7 @@
 time_step = 2.0
 filter_ratio = 4.0
 epsilon_den = 1e-06
-CHUNK_EDGES = (0, 8, 16, 24, 32)
+CHUNK_EDGES = (0, 8, 18, 26, 32)
 UNROLL = 4
 SLOTS = 4
 PARTS = 4
@@ -528,8 +528,6 @@
             )
     for copy in copies:
         copy.start()
-    for copy in copies:
-        copy.wait()
     m = mine * mb + lax.broadcasted_iota(jnp.int32, (kb, mb), 1)
     k = other * kb + lax.broadcasted_iota(jnp.int32, (kb, mb), 0)
     a = jnp.minimum(m, g.NTH - m).astype(jnp.float32)
@@ -549,7 +547,12 @@
         data[1, r, :kb, :] = im
         return cp, re, im
 
-    lax.fori_loop(0, R, forward, (zero, zero, zero), unroll=4)
+    state = (zero, zero, zero)
+    for c in range(g.chunks):
+        for copy in copies[c * g.ng : (c + 1) * g.ng]:
+            copy.wait()
+        start = g.ng * g.first[c]
+        state = lax.fori_loop(start, start + g.ng * g.rb[c], forward, state, unroll=4)
 
     def backward(i, carry):
         re, im = carry

time: 258 us -> 255 us (0.988)
  waiting for transfers between devices: 79.2 us -> 74.3 us
    ppermute x52, waiting for transfers between devices: 61.1 us -> 56.2 us  [exchange(): received.append(lax.ppermute(blocks[s], axis, ring))]
  transfers between devices with their start and end apart: 60 -> 60, of which waited for: 27 -> 19; matrix products, arithmetic and copies ran while one was open for 1% -> 1% of each run, Pallas kernels for 17% -> 17%
where the time goes in v3:
time: 255 us; the launch traced here: 251 us
  Pallas kernels  84.2 us (33%)
  waiting for transfers between devices  74.3 us (29%)
  starting transfers between devices  70.8 us (28%)
  blocking collectives  13.9 us (5%)
  local copies, waits for them, and re-layouts  4.65 us (2%)
    ppermute x52, starting transfers between devices, exchange(): received.append(lax.ppermute(blocks[s], axis, ring))  63.3 us
    ppermute x52, waiting for transfers between devices, exchange(): received.append(lax.ppermute(blocks[s], axis, ring))  56.2 us
    pallas_call x1, Pallas kernels, program(): pl.pallas_call(functools.partial(source_kernel, g), out_shape=[shape(T, Z...  22.6 us
    pallas_call x1, Pallas kernels, program(): pl.pallas_call(functools.partial(inner_kernel, g), out_shape=shape(2, 8,...  21.3 us
    ppermute x8, waiting for transfers between devices, move(): return lax.ppermute(block, ('theta', 'gz'), ring)  18.1 us
    all_to_all x1, blocking collectives, program(): lax.all_to_all(jnp.broadcast_to(part[None], (count, 8, R)), ('theta', 'gz...  13.9 us
    pallas_call x4, Pallas kernels, program(): pl.pallas_call(functools.partial(turn_kernel, g, rb), out_shape=[shape(2,...  13.7 us
    pallas_call x4, Pallas kernels, program(): pl.pallas_call(functools.partial(axial_kernel, g, rb), out_shape=[shape(r...  10.9 us
  transfers between devices with their start and end apart: 60, of which 19 were waited for; matrix products, arithmetic and copies ran while one was open for 1% of the time, Pallas kernels for 17%

profile of v3, /device:TPU:15, one launch (start us, length us, event | category | flops | bytes accessed | tf_op | source)
XLA Modules:
  0.0 250.9 jit_solution(4221278461521552897)
XLA Ops:
  6.9 3.2 %collective-permute-start.4 = (f32[3,3,3,128]{3,2,1,0:T(4,128)S(1)}, f32[3,3,3,128]{3,2,1,0:T(4,128)S(1)}, u32[]{:S(2)}, u32[]{:S(2)}) collective-permute-start(f32[3,3,3,128]{3,2,1,0:T(4,128)S(1)} %get-tuple-element.217), channel_id=1, source_target_pairs={{0,5},{1,6},{2,7},{3,4},{4,9},{5,10},{6,11},{7,8},{8,13},{9,14},{1... | collective-permute-start | bytes 41480 | tf_op jit(solution)/shard_map/ppermute | solution.py:608
  10.0 10.8 %collective-permute-done.4.refs_4_ = f32[3,3,3,128]{3,2,1,0:T(4,128)S(1)} collective-permute-done((f32[3,3,3,128]{3,2,1,0:T(4,128)S(1)}, f32[3,3,3,128]{3,2,1,0:T(4,128)S(1)}, u32[]{:S(2)}, u32[]{:S(2)}) %collective-permute-start.4) | collective-permute-done | bytes 13856 | tf_op jit(solution)/shard_map/ppermute | solution.py:608
  21.6 3.3 %collective-permute-done.5.refs_5_ = f32[3,3,3,128]{3,2,1,0:T(4,128)S(1)} collective-permute-done((f32[3,3,3,128]{3,2,1,0:T(4,128)S(1)}, f32[3,3,3,128]{3,2,1,0:T(4,128)S(1)}, u32[]{:S(2)}, u32[]{:S(2)}) %collective-permute-start.5) | collective-permute-done | bytes 13856 | tf_op jit(solution)/shard_map/ppermute | solution.py:608
  24.9 4.1 %collective-permute-done.6.refs_6_ = f32[3,3,3,128]{3,2,1,0:T(4,128)S(1)} collective-permute-done((f32[3,3,3,128]{3,2,1,0:T(4,128)S(1)}, f32[3,3,3,128]{3,2,1,0:T(4,128)S(1)}, u32[]{:S(2)}, u32[]{:S(2)}) %collective-permute-start.6) | collective-permute-done | bytes 13856 | tf_op jit(solution)/shard_map/ppermute | solution.py:608
  29.0 21.3 %inner_sums.1.refs_8_ = f32[2,8,128]{2,1,0:T(8,128)S(1)} custom-call(f32[3,64,64,128]{3,2,1,0:T(8,128)} %v.3), custom_call_target="tpu_custom_call" | custom-call | tf_op jit(solution)/shard_map/inner_sums/pallas_call | solution.py:676
  50.5 9.0 %edge_sums.1 = f32[8,128]{1,0:T(8,128)S(1)} custom-call(f32[3,64,64,128]{3,2,1,0:T(8,128)S(1)} %copy-done, f32[3,3,64,128]{3,2,1,0:T(8,128)S(1)} %collective-permute-done.refs_0_, f32[3,3,64,128]{3,2,1,0:T(8,128)S(1)} %collective-permute-done.1.refs_1_, f32[3,3,64,128]{3,2,1,0:T(8,128)S(1)} %collective-permute-done.2.refs_2_, ...), custom_call_target="tpu_custom_call" | custom-call | tf_op jit(solution)/shard_map/edge_sums/pallas_call | solution.py:685
  59.6 13.9 %all_to_all.5.refs_9_ = f32[32,8,128]{2,1,0:T(8,128)} all-to-all(f32[32,8,128]{2,1,0:T(8,128)S(1)} %broadcast_in_dim.2), channel_id=1, replica_groups=mesh['theta'=8,'gz'=4] {'theta','gz'}, dimensions={0} | all-to-all | bytes 262144 | tf_op jit(solution)/shard_map/all_to_all | solution.py:701
  73.5 22.6 %source.3 = (f32[64,64,128]{2,1,0:T(8,128)}, f32[8,32,128]{2,1,0:T(8,128)}, f32[8,32,128]{2,1,0:T(8,128)}, f32[8,32,128]{2,1,0:T(8,128)}, f32[8,32,128]{2,1,0:T(...) custom-call(f32[3,64,64,128]{3,2,1,0:T(8,128)} %v.3, ...), custom_call_target="tpu_custom_call" | custom-call | tf_op jit(solution)/shard_map/source/pallas_call | solution.py:704
  114.4 3.9 %collective-permute-start.13 = (f32[8,32,128]{2,1,0:T(8,128)S(1)}, f32[8,32,128]{2,1,0:T(8,128)S(1)}, u32[]{:S(2)}, u32[]{:S(2)}) collective-permute-start(f32[8,32,128]{2,1,0:T(8,128)S(1)} %get-tuple-element.123), channel_id=1, source_target_pairs={{0,12},{4,16},{8,20},{12,24},{16,28},{20,0},{24,4},{28,8},{1,13},{... | collective-permute-start | bytes 393224 | tf_op jit(solution)/shard_map/ppermute | solution.py:590
  123.3 3.4 %axial_modes.5 = (f32[10,32,128]{2,1,0:T(8,128)S(1)}, f32[10,32,128]{2,1,0:T(8,128)S(1)}, f32[10,32,128]{2,1,0:T(8,128)S(1)}, f32[10,32,128]{2,1,0:T(8,128)S(1)}...) custom-call(f32[10,32,128]{2,1,0:T(8,128)S(1)} %copy-done.8, ...), custom_call_target="tpu_custom_call" | custom-call | tf_op jit(solution)/shard_map/axial_modes/pallas_call | solution.py:733
  130.3 4.8 %collective-permute-done.14.refs_4_ = f32[8,32,128]{2,1,0:T(8,128)S(1)} collective-permute-done((f32[8,32,128]{2,1,0:T(8,128)S(1)}, f32[8,32,128]{2,1,0:T(8,128)S(1)}, u32[]{:S(2)}, u32[]{:S(2)}) %collective-permute-start.14) | collective-permute-done | bytes 131104 | tf_op jit(solution)/shard_map/ppermute | solution.py:590
  146.7 3.4 %turn_modes.4 = (f32[2,8,32,128]{3,2,1,0:T(8,128)S(1)}, f32[2,8,32,128]{3,2,1,0:T(8,128)S(1)}, f32[2,8,32,128]{3,2,1,0:T(8,128)S(1)}, f32[2,8,32,128]{3,2,1,0:T(8,128)S(1)}) custom-call(f32[8,32,128]{2,1,0:T(8,128)S(1)} %get-tuple-element.120.refs_0_, f32[8,32,128]{2,1,0:T(8,128)S(1)} %collective-permute-done.11.refs_1_, ...), custom_call_target="tpu_custom_call" | custom-call | tf_op jit(solution)/shard_map/turn_modes/pallas_call | solution.py:745
  152.5 6.7 %collective-permute-done.26.refs_3_ = f32[10,32,128]{2,1,0:T(8,128)S(1)} collective-permute-done((f32[10,32,128]{2,1,0:T(8,128)S(1)}, f32[10,32,128]{2,1,0:T(8,128)S(1)}, u32[]{:S(2)}, u32[]{:S(2)}) %collective-permute-start.26) | collective-permute-done | bytes 163872 | tf_op jit(solution)/shard_map/ppermute | solution.py:590
  172.1 3.5 %collective-permute-start.38 = (f32[8,32,128]{2,1,0:T(8,128)S(1)}, f32[8,32,128]{2,1,0:T(8,128)S(1)}, u32[]{:S(2)}, u32[]{:S(2)}) collective-permute-start(f32[8,32,128]{2,1,0:T(8,128)S(1)} %get-tuple-element.178), channel_id=1, source_target_pairs={{0,8},{4,12},{8,16},{12,20},{16,24},{20,28},{24,0},{28,4},{1,9},{5... | collective-permute-start | bytes 393224 | tf_op jit(solution)/shard_map/ppermute | solution.py:590
  176.8 3.1 %collective-permute-start.40 = (f32[8,32,128]{2,1,0:T(8,128)S(1)}, f32[8,32,128]{2,1,0:T(8,128)S(1)}, u32[]{:S(2)}, u32[]{:S(2)}) collective-permute-start(f32[8,32,128]{2,1,0:T(8,128)S(1)} %get-tuple-element.180), channel_id=1, source_target_pairs={{0,16},{4,20},{8,24},{12,28},{16,0},{20,4},{24,8},{28,12},{1,17},{... | collective-permute-start | bytes 393224 | tf_op jit(solution)/shard_map/ppermute | solution.py:590
  186.4 8.0 %collective-permute-done.40.refs_4_ = f32[8,32,128]{2,1,0:T(8,128)S(1)} collective-permute-done((f32[8,32,128]{2,1,0:T(8,128)S(1)}, f32[8,32,128]{2,1,0:T(8,128)S(1)}, u32[]{:S(2)}, u32[]{:S(2)}) %collective-permute-start.40) | collective-permute-done | bytes 131104 | tf_op jit(solution)/shard_map/ppermute | solution.py:590
  194.4 3.4 %collective-permute-start.52 = (f32[6,32,128]{2,1,0:T(8,128)S(1)}, f32[6,32,128]{2,1,0:T(8,128)S(1)}, u32[]{:S(2)}, u32[]{:S(2)}) collective-permute-start(f32[6,32,128]{2,1,0:T(8,128)S(1)} %get-tuple-element.195), channel_id=1, source_target_pairs={{0,12},{4,16},{8,20},{12,24},{16,28},{20,0},{24,4},{28,8},{1,13},{... | collective-permute-start | bytes 294920 | tf_op jit(solution)/shard_map/ppermute | solution.py:590
  197.8 4.2 %turn_modes.5 = (f32[2,10,32,128]{3,2,1,0:T(8,128)S(1)}, f32[2,10,32,128]{3,2,1,0:T(8,128)S(1)}, f32[2,10,32,128]{3,2,1,0:T(8,128)S(1)}, f32[2,10,32,128]{3,2,1,0:T(8,128)S(1)}) custom-call(f32[10,32,128]{2,1,0:T(8,128)S(1)} %get-tuple-element.148.refs_0_, f32[10,32,128]{2,1,0:T(8,128)S(1)} %collective-permute-done.24.refs_1_, ...), custom_call_target="tpu_custom_call" | custom-call | tf_op jit(solution)/shard_map/turn_modes/pallas_call | solution.py:745
  209.2 4.1 %collective-permute-done.53.refs_4_ = f32[6,32,128]{2,1,0:T(8,128)S(1)} collective-permute-done((f32[6,32,128]{2,1,0:T(8,128)S(1)}, f32[6,32,128]{2,1,0:T(8,128)S(1)}, u32[]{:S(2)}, u32[]{:S(2)}) %collective-permute-start.53) | collective-permute-done | bytes 98336 | tf_op jit(solution)/shard_map/ppermute | solution.py:590
  214.5 3.4 %turn_modes.6 = (f32[2,8,32,128]{3,2,1,0:T(8,128)S(1)}, f32[2,8,32,128]{3,2,1,0:T(8,128)S(1)}, f32[2,8,32,128]{3,2,1,0:T(8,128)S(1)}, f32[2,8,32,128]{3,2,1,0:T(8,128)S(1)}) custom-call(f32[8,32,128]{2,1,0:T(8,128)S(1)} %get-tuple-element.176.refs_0_, f32[8,32,128]{2,1,0:T(8,128)S(1)} %collective-permute-done.37.refs_1_, ...), custom_call_target="tpu_custom_call" | custom-call | tf_op jit(solution)/shard_map/turn_modes/pallas_call | solution.py:745
  219.7 2.9 %collective-permute-done.56.refs_7_ = f32[6,32,128]{2,1,0:T(8,128)S(1)} collective-permute-done((f32[6,32,128]{2,1,0:T(8,128)S(1)}, f32[6,32,128]{2,1,0:T(8,128)S(1)}, u32[]{:S(2)}, u32[]{:S(2)}) %collective-permute-start.56) | collective-permute-done | bytes 98336 | tf_op jit(solution)/shard_map/ppermute | solution.py:590
  229.5 7.3 %collective-permute-done.45.refs_10_ = f32[2,8,32,128]{3,2,1,0:T(8,128)S(1)} collective-permute-done((f32[2,8,32,128]{3,2,1,0:T(8,128)S(1)}, f32[2,8,32,128]{3,2,1,0:T(8,128)S(1)}, u32[]{:S(2)}, u32[]{:S(2)}) %collective-permute-start.45) | collective-permute-done | bytes 262176 | tf_op jit(solution)/shard_map/ppermute | solution.py:590
  236.8 7.4 %collective-permute-done.58.refs_14_ = f32[2,6,32,128]{3,2,1,0:T(8,128)S(1)} collective-permute-done((f32[2,6,32,128]{3,2,1,0:T(8,128)S(1)}, f32[2,6,32,128]{3,2,1,0:T(8,128)S(1)}, u32[]{:S(2)}, u32[]{:S(2)}) %collective-permute-start.58) | collective-permute-done | bytes 196640 | tf_op jit(solution)/shard_map/ppermute | solution.py:590
  244.1 6.7 %solve_modes.1 = f32[2,128,32,128]{3,2,1,0:T(8,128)} custom-call(f32[2,8,32,128]{3,2,1,0:T(8,128)S(1)} %get-tuple-element.128.refs_0_, f32[2,8,32,128]{3,2,1,0:T(8,128)S(1)} %collective-permute-done.18.refs_1_, f32[2,8,32,128]{3,2,1,0:T(8,128)S(1)} %collective-permute-done.19.refs_2_, f32[2,8,32,128]{3,2,1,0:T(8,128)S(1)} %collective-permute-done.20.refs_3_, ...), custom_call_target="tpu_custom_call" | custom-call | tf_op jit(solution)/shard_map/solve_modes/pallas_call | solution.py:754
  (171 shorter events, 85.3 us)
Async XLA Ops:
  1.7 48.6 %collective-permute-start = (f32[3,3,64,128]{3,2,1,0:T(8,128)S(1)}, f32[3,3,64,128]{3,2,1,0:T(8,128)S(1)}, u32[]{:S(2)}, u32[]{:S(2)}) collective-permute-start(f32[3,3,64,128]{3,2,1,0:T(8,128)S(1)} %get-tuple-element.207), channel_id=1, source_target_pairs={{0,4},{1,5},{2,6},{3,7},{4,8},{5,9},{6,10},{7,11},{8,12},{9,13},{1... | collective-permute-start | bytes 884744 | tf_op jit(solution)/shard_map/ppermute | solution.py:608
  3.6 46.7 %collective-permute-start.1 = (f32[3,3,64,128]{3,2,1,0:T(8,128)S(1)}, f32[3,3,64,128]{3,2,1,0:T(8,128)S(1)}, u32[]{:S(2)}, u32[]{:S(2)}) collective-permute-start(f32[3,3,64,128]{3,2,1,0:T(8,128)S(1)} %get-tuple-element.206), channel_id=1, source_target_pairs={{0,28},{1,29},{2,30},{3,31},{4,0},{5,1},{6,2},{7,3},{8,4},{9,5},{1... | collective-permute-start | bytes 884744 | tf_op jit(solution)/shard_map/ppermute | solution.py:608
  5.2 45.1 %collective-permute-start.2 = (f32[3,3,64,128]{3,2,1,0:T(8,128)S(1)}, f32[3,3,64,128]{3,2,1,0:T(8,128)S(1)}, u32[]{:S(2)}, u32[]{:S(2)}) collective-permute-start(f32[3,3,64,128]{3,2,1,0:T(8,128)S(1)} %bitcast.6), channel_id=1, source_target_pairs={{0,1},{1,2},{2,3},{3,0},{4,5},{5,6},{6,7},{7,4},{8,9},{9,10},{10,1... | collective-permute-start | bytes 884744 | tf_op jit(solution)/shard_map/ppermute | solution.py:608
  5.5 44.9 %collective-permute-start.3 = (f32[3,3,64,128]{3,2,1,0:T(8,128)S(1)}, f32[3,3,64,128]{3,2,1,0:T(8,128)S(1)}, u32[]{:S(2)}, u32[]{:S(2)}) collective-permute-start(f32[3,3,64,128]{3,2,1,0:T(8,128)S(1)} %bitcast.8), channel_id=1, source_target_pairs={{0,3},{1,0},{2,1},{3,2},{4,7},{5,4},{6,5},{7,6},{8,11},{9,8},{10,9... | collective-permute-start | bytes 884744 | tf_op jit(solution)/shard_map/ppermute | solution.py:608
  29.0 21.4 %collective-permute-start.7 = (f32[3,3,3,128]{3,2,1,0:T(4,128)S(1)}, f32[3,3,3,128]{3,2,1,0:T(4,128)S(1)}, u32[]{:S(2)}, u32[]{:S(2)}) collective-permute-start(f32[3,3,3,128]{3,2,1,0:T(4,128)S(1)} %get-tuple-element.214), channel_id=1, source_target_pairs={{0,31},{1,28},{2,29},{3,30},{4,3},{5,0},{6,1},{7,2},{8,7},{9,4},{1... | collective-permute-start | bytes 41480 | tf_op jit(solution)/shard_map/ppermute | solution.py:608
  110.9 15.7 %collective-permute-start.11 = (f32[8,32,128]{2,1,0:T(8,128)S(1)}, f32[8,32,128]{2,1,0:T(8,128)S(1)}, u32[]{:S(2)}, u32[]{:S(2)}) collective-permute-start(f32[8,32,128]{2,1,0:T(8,128)S(1)} %get-tuple-element.121), channel_id=1, source_target_pairs={{0,4},{4,8},{8,12},{12,16},{16,20},{20,24},{24,28},{28,0},{1,5},{5... | collective-permute-start | bytes 393224 | tf_op jit(solution)/shard_map/ppermute | solution.py:590
  113.4 15.6 %collective-permute-start.12 = (f32[8,32,128]{2,1,0:T(8,128)S(1)}, f32[8,32,128]{2,1,0:T(8,128)S(1)}, u32[]{:S(2)}, u32[]{:S(2)}) collective-permute-start(f32[8,32,128]{2,1,0:T(8,128)S(1)} %get-tuple-element.122), channel_id=1, source_target_pairs={{0,8},{4,12},{8,16},{12,20},{16,24},{20,28},{24,0},{28,4},{1,9},{5... | collective-permute-start | bytes 393224 | tf_op jit(solution)/shard_map/ppermute | solution.py:590
  118.3 16.9 %collective-permute-start.14 = (f32[8,32,128]{2,1,0:T(8,128)S(1)}, f32[8,32,128]{2,1,0:T(8,128)S(1)}, u32[]{:S(2)}, u32[]{:S(2)}) collective-permute-start(f32[8,32,128]{2,1,0:T(8,128)S(1)} %get-tuple-element.124), channel_id=1, source_target_pairs={{0,16},{4,20},{8,24},{12,28},{16,0},{20,4},{24,8},{28,12},{1,17},{... | collective-permute-start | bytes 393224 | tf_op jit(solution)/shard_map/ppermute | solution.py:590
  119.6 17.0 %collective-permute-start.15 = (f32[8,32,128]{2,1,0:T(8,128)S(1)}, f32[8,32,128]{2,1,0:T(8,128)S(1)}, u32[]{:S(2)}, u32[]{:S(2)}) collective-permute-start(f32[8,32,128]{2,1,0:T(8,128)S(1)} %get-tuple-element.125), channel_id=1, source_target_pairs={{0,20},{4,24},{8,28},{12,0},{16,4},{20,8},{24,12},{28,16},{1,21},{... | collective-permute-start | bytes 393224 | tf_op jit(solution)/shard_map/ppermute | solution.py:590
  141.3 17.9 %collective-permute-start.26 = (f32[10,32,128]{2,1,0:T(8,128)S(1)}, f32[10,32,128]{2,1,0:T(8,128)S(1)}, u32[]{:S(2)}, u32[]{:S(2)}) collective-permute-start(f32[10,32,128]{2,1,0:T(8,128)S(1)} %get-tuple-element.151), channel_id=1, source_target_pairs={{0,12},{4,16},{8,20},{12,24},{16,28},{20,0},{24,4},{28,8},{1,13},{... | collective-permute-start | bytes 491528 | tf_op jit(solution)/shard_map/ppermute | solution.py:590
  143.4 19.3 %collective-permute-start.27 = (f32[10,32,128]{2,1,0:T(8,128)S(1)}, f32[10,32,128]{2,1,0:T(8,128)S(1)}, u32[]{:S(2)}, u32[]{:S(2)}) collective-permute-start(f32[10,32,128]{2,1,0:T(8,128)S(1)} %get-tuple-element.152), channel_id=1, source_target_pairs={{0,16},{4,20},{8,24},{12,28},{16,0},{20,4},{24,8},{28,12},{1,17},{... | collective-permute-start | bytes 491528 | tf_op jit(solution)/shard_map/ppermute | solution.py:590
  145.3 19.0 %collective-permute-start.28 = (f32[10,32,128]{2,1,0:T(8,128)S(1)}, f32[10,32,128]{2,1,0:T(8,128)S(1)}, u32[]{:S(2)}, u32[]{:S(2)}) collective-permute-start(f32[10,32,128]{2,1,0:T(8,128)S(1)} %get-tuple-element.153), channel_id=1, source_target_pairs={{0,20},{4,24},{8,28},{12,0},{16,4},{20,8},{24,12},{28,16},{1,21},{... | collective-permute-start | bytes 491528 | tf_op jit(solution)/shard_map/ppermute | solution.py:590
  150.1 21.4 %collective-permute-start.18 = (f32[2,8,32,128]{3,2,1,0:T(8,128)S(1)}, f32[2,8,32,128]{3,2,1,0:T(8,128)S(1)}, u32[]{:S(2)}, u32[]{:S(2)}) collective-permute-start(f32[2,8,32,128]{3,2,1,0:T(8,128)S(1)} %get-tuple-element.129), channel_id=1, source_target_pairs={{0,1},{1,2},{2,3},{3,0},{4,5},{5,6},{6,7},{7,4},{8,9},{9,10},{10,1... | collective-permute-start | bytes 786440 | tf_op jit(solution)/shard_map/ppermute | solution.py:590
  151.2 20.5 %collective-permute-start.19 = (f32[2,8,32,128]{3,2,1,0:T(8,128)S(1)}, f32[2,8,32,128]{3,2,1,0:T(8,128)S(1)}, u32[]{:S(2)}, u32[]{:S(2)}) collective-permute-start(f32[2,8,32,128]{3,2,1,0:T(8,128)S(1)} %get-tuple-element.130), channel_id=1, source_target_pairs={{0,2},{1,3},{2,0},{3,1},{4,6},{5,7},{6,4},{7,5},{8,10},{9,11},{10,... | collective-permute-start | bytes 786440 | tf_op jit(solution)/shard_map/ppermute | solution.py:590
  176.8 17.6 %collective-permute-start.40 = (f32[8,32,128]{2,1,0:T(8,128)S(1)}, f32[8,32,128]{2,1,0:T(8,128)S(1)}, u32[]{:S(2)}, u32[]{:S(2)}) collective-permute-start(f32[8,32,128]{2,1,0:T(8,128)S(1)} %get-tuple-element.180), channel_id=1, source_target_pairs={{0,16},{4,20},{8,24},{12,28},{16,0},{20,4},{24,8},{28,12},{1,17},{... | collective-permute-start | bytes 393224 | tf_op jit(solution)/shard_map/ppermute | solution.py:590
  179.9 24.8 %collective-permute-start.42 = (f32[8,32,128]{2,1,0:T(8,128)S(1)}, f32[8,32,128]{2,1,0:T(8,128)S(1)}, u32[]{:S(2)}, u32[]{:S(2)}) collective-permute-start(f32[8,32,128]{2,1,0:T(8,128)S(1)} %get-tuple-element.182), channel_id=1, source_target_pairs={{0,24},{4,28},{8,0},{12,4},{16,8},{20,12},{24,16},{28,20},{1,25},{... | collective-permute-start | bytes 393224 | tf_op jit(solution)/shard_map/ppermute | solution.py:590
  182.5 24.2 %collective-permute-start.43 = (f32[8,32,128]{2,1,0:T(8,128)S(1)}, f32[8,32,128]{2,1,0:T(8,128)S(1)}, u32[]{:S(2)}, u32[]{:S(2)}) collective-permute-start(f32[8,32,128]{2,1,0:T(8,128)S(1)} %get-tuple-element.183), channel_id=1, source_target_pairs={{0,28},{4,0},{8,4},{12,8},{16,12},{20,16},{24,20},{28,24},{1,29},{... | collective-permute-start | bytes 393224 | tf_op jit(solution)/shard_map/ppermute | solution.py:590
  184.6 22.3 %collective-permute-start.50 = (f32[6,32,128]{2,1,0:T(8,128)S(1)}, f32[6,32,128]{2,1,0:T(8,128)S(1)}, u32[]{:S(2)}, u32[]{:S(2)}) collective-permute-start(f32[6,32,128]{2,1,0:T(8,128)S(1)} %get-tuple-element.193), channel_id=1, source_target_pairs={{0,4},{4,8},{8,12},{12,16},{16,20},{20,24},{24,28},{28,0},{1,5},{5... | collective-permute-start | bytes 294920 | tf_op jit(solution)/shard_map/ppermute | solution.py:590
  194.4 14.8 %collective-permute-start.52 = (f32[6,32,128]{2,1,0:T(8,128)S(1)}, f32[6,32,128]{2,1,0:T(8,128)S(1)}, u32[]{:S(2)}, u32[]{:S(2)}) collective-permute-start(f32[6,32,128]{2,1,0:T(8,128)S(1)} %get-tuple-element.195), channel_id=1, source_target_pairs={{0,12},{4,16},{8,20},{12,24},{16,28},{20,0},{24,4},{28,8},{1,13},{... | collective-permute-start | bytes 294920 | tf_op jit(solution)/shard_map/ppermute | solution.py:590
  204.7 18.2 %collective-permute-start.31 = (f32[2,10,32,128]{3,2,1,0:T(8,128)S(1)}, f32[2,10,32,128]{3,2,1,0:T(8,128)S(1)}, u32[]{:S(2)}, u32[]{:S(2)}) collective-permute-start(f32[2,10,32,128]{3,2,1,0:T(8,128)S(1)} %get-tuple-element.157), channel_id=1, source_target_pairs={{0,1},{1,2},{2,3},{3,0},{4,5},{5,6},{6,7},{7,4},{8,9},{9,10},{10,1... | collective-permute-start | bytes 983048 | tf_op jit(solution)/shard_map/ppermute | solution.py:590
  208.8 18.1 %collective-permute-start.32 = (f32[2,10,32,128]{3,2,1,0:T(8,128)S(1)}, f32[2,10,32,128]{3,2,1,0:T(8,128)S(1)}, u32[]{:S(2)}, u32[]{:S(2)}) collective-permute-start(f32[2,10,32,128]{3,2,1,0:T(8,128)S(1)} %get-tuple-element.158), channel_id=1, source_target_pairs={{0,2},{1,3},{2,0},{3,1},{4,6},{5,7},{6,4},{7,5},{8,10},{9,11},{10,... | collective-permute-start | bytes 983048 | tf_op jit(solution)/shard_map/ppermute | solution.py:590
  209.2 18.8 %collective-permute-start.33 = (f32[2,10,32,128]{3,2,1,0:T(8,128)S(1)}, f32[2,10,32,128]{3,2,1,0:T(8,128)S(1)}, u32[]{:S(2)}, u32[]{:S(2)}) collective-permute-start(f32[2,10,32,128]{3,2,1,0:T(8,128)S(1)} %get-tuple-element.159), channel_id=1, source_target_pairs={{0,3},{1,0},{2,1},{3,2},{4,7},{5,4},{6,5},{7,6},{8,11},{9,8},{10,9... | collective-permute-start | bytes 983048 | tf_op jit(solution)/shard_map/ppermute | solution.py:590
  228.0 16.1 %collective-permute-start.58 = (f32[2,6,32,128]{3,2,1,0:T(8,128)S(1)}, f32[2,6,32,128]{3,2,1,0:T(8,128)S(1)}, u32[]{:S(2)}, u32[]{:S(2)}) collective-permute-start(f32[2,6,32,128]{3,2,1,0:T(8,128)S(1)} %get-tuple-element.202), channel_id=1, source_target_pairs={{0,2},{1,3},{2,0},{3,1},{4,6},{5,7},{6,4},{7,5},{8,10},{9,11},{10,... | collective-permute-start | bytes 589832 | tf_op jit(solution)/shard_map/ppermute | solution.py:590
  229.1 15.0 %collective-permute-start.59 = (f32[2,6,32,128]{3,2,1,0:T(8,128)S(1)}, f32[2,6,32,128]{3,2,1,0:T(8,128)S(1)}, u32[]{:S(2)}, u32[]{:S(2)}) collective-permute-start(f32[2,6,32,128]{3,2,1,0:T(8,128)S(1)} %get-tuple-element.203), channel_id=1, source_target_pairs={{0,3},{1,0},{2,1},{3,2},{4,7},{5,4},{6,5},{7,6},{8,11},{9,8},{10,9... | collective-permute-start | bytes 589832 | tf_op jit(solution)/shard_map/ppermute | solution.py:590
  (62 other events, 1209.0 us)
